TPU v7x, 32 devices: a whole 2x2x4 slice. The times are simulated.
32 devices in a mesh: section: 2 (over core), dp: 4 (over z), mp: 4 (over y, x).
Axes of the slice: x: 2, y: 2, z: 4, core: 2. Of those that a mesh axis runs over, the one named last changes fastest.
Arguments:
- block_input: bfloat16 [8, 1024, 1024], P('dp', None, 'mp'), may hold values from -6 to 6
- cotangent: bfloat16 [8, 1024, 1024], P('dp', None, 'mp'), may hold values from -6 to 6
- lengths: int32 [8], P('dp'), may hold values from 1 to 1024, 5120 in all
- ln_gain: float32 [2, 1024], P('section'), may hold values from 0.5 to 1.5
- ln_bias: float32 [2, 1024], P('section'), may hold values from -2 to 2
- w_qkv: bfloat16 [2, 3, 1024, 1024], P('section', None, None, 'mp'), may hold values from -0.1875 to 0.1875
- w_out: bfloat16 [2, 1024, 1024], P('section', 'mp'), may hold values from -1.5 to 1.5
- w_up: bfloat16 [2, 1024, 4096], P('section', None, 'mp'), may hold values from -0.1875 to 0.1875
- w_down: bfloat16 [2, 4096, 1024], P('section', 'mp'), may hold values from -0.09375 to 0.09375
- freq_table: bfloat16 [2, 16, 64, 64], P('section', 'mp'), may hold values from -0.75 to 0.75
- feat_weight: float32 [2, 16, 64], P('section', 'mp'), may hold values from 0.5 to 2
Outputs:
- boundary: float32 [2, 8, 1024, 1024], P('section', 'dp', None, 'mp')
- gain_grad: float32 [2, 1024], P('section', 'mp')
- bias_grad: float32 [2, 1024], P('section', 'mp')
- qkv_grad: float32 [2, 3, 1024, 1024], P('section', None, 'dp', 'mp')
- out_grad: float32 [2, 1024, 1024], P('section', 'mp', 'dp')
- up_grad: float32 [2, 1024, 4096], P('section', 'dp', 'mp')
- down_grad: float32 [2, 4096, 1024], P('section', 'mp', 'dp')
- freq_grad: float32 [2, 16, 64, 64], P('section', 'mp')
- feat_grad: float32 [2, 16, 64], P('section', 'mp')
Inputs may be any that keep to these rules, and one draw needn't show every extreme that they name: Slot n holds lengths[n] real tokens at its start; later positions are padding.
All inputs are finite; a program needn't handle non-finite values. No bound on the sum of `lengths` on one device may be relied on, other than what follows from the above.
Results may differ from a plain program's by a relative error of at most 0.03.
Values may be sent and summed in bfloat16 or wider, within the bound.
No kernel may reach another device: no remote copies, remote signals or barrier semaphores. Data moves between devices by JAX's collectives and lax.ppermute only.
A program may use at most 384 MiB of HBM per device.

v0:
```python
import functools
import math

import jax
import jax.numpy as jnp
from jax import lax
from jax.experimental import pallas as pl
from jax.experimental.pallas import tpu as pltpu
from jax.sharding import PartitionSpec as P

ROT = 16
TILE = 256
HEAD = 64
LANES = 256
EPS = 1e-05
F32 = jnp.float32
BF16 = jnp.bfloat16
RSQRT2 = math.sqrt(0.5)
RSQRT2PI = 1.0 / math.sqrt(2.0 * math.pi)
SAVED = 14


def dot_nn(a, b):
    return lax.dot_general(a, b, (((1,), (0,)), ((), ())), preferred_element_type=F32)


def dot_nt(a, b):
    return lax.dot_general(a, b, (((1,), (1,)), ((), ())), preferred_element_type=F32)


def dot_tn(a, b):
    return lax.dot_general(a, b, (((0,), (0,)), ((), ())), preferred_element_type=F32)


def split(values):
    high = values.astype(BF16)
    return high, (values - high.astype(F32)).astype(BF16)


def iota(shape, dim):
    return lax.broadcasted_iota(jnp.int32, shape, dim)


def partner(values):
    later = pltpu.roll(values, LANES - ROT // 2, 1)
    earlier = pltpu.roll(values, ROT // 2, 1)
    lower = iota(values.shape, 1) % HEAD < ROT // 2
    return jnp.where(lower, later, earlier)


def twice(table):
    return jnp.concatenate([table, table], axis=1)


def head_of(shape, dim):
    return iota(shape, dim) // HEAD


def weight_copies(refs, w_in, w_out, sems, which):
    qkv, up, out, down = refs
    ends = [(qkv.at[0, t], w_in.at[:, t * LANES:(t + 1) * LANES]) for t in range(3)] + [
        (up.at[0], w_in.at[:, 3 * LANES:]), (out.at[0], w_out.at[0:LANES, :]), (down.at[0], w_out.at[LANES:, :])]
    return [pltpu.make_async_copy(*ends[i], sems.at[i]) for i in which]


def start_weights(meta, mine, other, w_in, w_out, sems, order):
    def start(refs):
        for copy in weight_copies(refs, w_in, w_out, sems, order):
            copy.start()

    @pl.when(meta[1] == 1)
    def _():
        start(mine)

    @pl.when(meta[1] != 1)
    def _():
        start(other)


def wait_weights(step, refs, w_in, w_out, sems, which):
    @pl.when(step == 0)
    def _():
        for copy in weight_copies(refs, w_in, w_out, sems, which):
            copy.wait()


def forward_kernel(carried, phased, *refs):
    refs = list(refs)
    take = lambda n: [refs.pop(0) for _ in range(n)]
    meta, lens = take(2)
    p0, p1, p2, p3a, p3b, gain, bias, mix_hi, mix_lo, feat_w, cos_t, sin_t = take(12)
    mine, other = take(4), take(4)
    if carried:
        state_in, ksum_in = take(2)
        take(SAVED)
    parts = take(5 if phased else 4)
    normed, xhat, rstd, rq_o, rk_o, qf_o, kf_o, v_o, hcat, dgelu, invz, att_o, prior_s, prior_k = take(SAVED)
    state, ksum, w_in, w_out, sems = take(5)
    tile = pl.program_id(0)
    rank = meta[0]
    half = LANES // 2

    @pl.when(tile == 0)
    def _():
        start_weights(meta, mine, other, w_in, w_out, sems, (0, 1, 2, 3, 4, 5))
        if carried:
            state[...] = state_in[...]
            ksum[...] = ksum_in[...]
        else:
            state[...] = jnp.zeros_like(state)
            ksum[...] = jnp.zeros_like(ksum)

    pieces = [p0[...].astype(F32), p1[...].astype(F32), p2[...].astype(F32),
              jnp.concatenate([p3a[...], p3b[...]], axis=1).astype(F32)]
    width = 4 * LANES
    mean = jnp.sum(pieces[0] + pieces[1] + pieces[2] + pieces[3], axis=1, keepdims=True) * (1.0 / width)
    pieces = [piece - mean for piece in pieces]
    squares = sum(piece * piece for piece in pieces)
    factor = lax.rsqrt(jnp.sum(squares, axis=1, keepdims=True) * (1.0 / width) + EPS)
    for r in range(4):
        at = pl.ds(pl.multiple_of((rank ^ r) * LANES, LANES), LANES)
        hat = pieces[r] * factor
        if r == 0:
            xhat[...] = hat
        normed[:, at] = (hat * gain[:, at] + bias[:, at]).astype(BF16)
    rstd[...] = jnp.broadcast_to(factor, (TILE, half))
    tokens = normed[...]

    wait_weights(tile, mine, w_in, w_out, sems, (0, 1, 2))
    cosine, sine = twice(cos_t[...]), twice(sin_t[...])
    query = dot_nn(tokens, w_in[:, 0:LANES])
    key = dot_nn(tokens, w_in[:, LANES:2 * LANES])
    value = dot_nn(tokens, w_in[:, 2 * LANES:3 * LANES]).astype(BF16)
    rq = query * cosine + partner(query) * sine
    rk = key * cosine + partner(key) * sine
    weight = feat_w[...]

    def logits(rows):
        high, low = split(rows)
        return dot_nn(high, mix_hi[...]) + dot_nn(low, mix_hi[...]) + dot_nn(high, mix_lo[...])

    positions = lens[1] + tile * TILE + iota((TILE, LANES), 0)
    real = (positions < lens[0]).astype(F32)
    qf = (weight * jnp.exp(logits(rq))).astype(BF16)
    kf = (weight * jnp.exp(logits(rk)) * real).astype(BF16)
    rq_o[...] = rq.astype(BF16)
    rk_o[...] = rk.astype(BF16)
    qf_o[...] = qf
    kf_o[...] = kf
    v_o[...] = value

    square = (TILE, TILE)
    lower = iota(square, 0) >= iota(square, 1)
    same = head_of(square, 0) == head_of(square, 1)
    cumulative = dot_nn(lower.astype(BF16), kf) + ksum[0:1, :]
    high, low = split(qf.astype(F32) * cumulative)
    ones = same.astype(BF16)
    inverse = 1.0 / (dot_nn(high, ones) + dot_nn(low, ones))
    prior = jnp.where(same, state[...], 0.0)
    prior_hi, prior_lo = split(prior)
    numer = dot_nn(qf, prior_hi) + dot_nn(qf, prior_lo)
    lane_head = head_of((TILE, LANES), 1)
    zero = jnp.zeros((TILE, LANES), BF16)
    for h in range(LANES // HEAD):
        here = lane_head == h
        scores = dot_nt(qf, jnp.where(here, kf, zero))
        scores = jnp.where(lower, scores, 0.0).astype(BF16)
        numer = numer + dot_nn(scores, jnp.where(here, value, zero))
    prior_s[0] = prior
    prior_k[0] = ksum[...]
    state[...] = state[...] + dot_tn(kf, value)
    ksum[...] = jnp.broadcast_to(cumulative[TILE - 1:TILE, :], ksum.shape)
    invz[...] = inverse
    attended = numer * inverse
    att_o[...] = attended
    hcat[:, 0:LANES] = attended.astype(BF16)

    wait_weights(tile, mine, w_in, w_out, sems, (3,))
    for c in range(4):
        cols = slice(c * LANES, (c + 1) * LANES)
        up = dot_nn(tokens, w_in[:, (3 + c) * LANES:(4 + c) * LANES])
        cdf = 0.5 * (1.0 + lax.erf(up * RSQRT2))
        hcat[:, (1 + c) * LANES:(2 + c) * LANES] = (up * cdf).astype(BF16)
        dgelu[:, cols] = (cdf + up * (RSQRT2PI * jnp.exp(-0.5 * up * up))).astype(BF16)

    wait_weights(tile, mine, w_in, w_out, sems, (4, 5))
    hidden = hcat[...]
    emit(rank, lambda at: dot_nn(hidden, w_out[:, at]), parts)


def emit(rank, product, parts):
    half = LANES // 2
    for r in range(4):
        at = pl.ds(pl.multiple_of((rank ^ r) * LANES, LANES), LANES)
        part = product(at)
        if len(parts) == 4:
            parts[r][...] = part.astype(parts[r].dtype)
            continue
        sx, sy, k0, ka, kb = parts
        if r == 0:
            k0[...] = part
        elif r == 1:
            sx[0] = part[:, :half].astype(BF16)
            kb[...] = part[:, half:]
        elif r == 2:
            ka[...] = part[:, :half]
            sy[0] = part[:, half:].astype(BF16)
        else:
            sx[1] = part[:, :half].astype(BF16)
            sy[1] = part[:, half:].astype(BF16)


def backward_kernel(carried, phased, *refs):
    refs = list(refs)
    take = lambda n: [refs.pop(0) for _ in range(n)]
    meta, = take(1)
    grad, normed, rq, rk, qf_i, kf_i, v_i, att_i, dgelu, invz, prior_s, prior_k, gain, bias, mix_hi, cos_t, sin_t = take(17)
    mine, other = take(4), take(4)
    if carried:
        state_in, gsum_in, dmix_in, fsum_in = take(4)
        take(2)
    parts = take(5 if phased else 4)
    stats, dcat, state, gsum, dmix, fsum = take(6)
    w_in, w_out, sems = take(3)
    step = pl.program_id(0)
    rank = meta[0]

    @pl.when(step == 0)
    def _():
        start_weights(meta, mine, other, w_in, w_out, sems, (4, 5, 0, 1, 2, 3))
        if carried:
            state[...] = state_in[...]
            gsum[...] = gsum_in[...]
            dmix[...] = dmix_in[...]
            fsum[...] = fsum_in[...]
        else:
            state[...] = jnp.zeros_like(state)
            gsum[...] = jnp.zeros_like(gsum)
            dmix[...] = jnp.zeros_like(dmix)
            fsum[...] = jnp.zeros_like(fsum)

    wait_weights(step, mine, w_in, w_out, sems, (4, 5))
    g = grad[...]
    d_att = dot_nt(g, w_out[0:LANES, :]).astype(BF16).astype(F32)
    square = (TILE, TILE)
    same = head_of(square, 0) == head_of(square, 1)
    ones = same.astype(BF16)
    inverse = invz[...]
    dn = (d_att * inverse).astype(BF16)
    dn32 = dn.astype(F32)
    high, low = split(dn32 * att_i[...])
    dden = -(dot_nn(high, ones) + dot_nn(low, ones))
    den_hi = dden.astype(BF16).astype(F32)
    roll_hi = pltpu.roll(den_hi, HEAD, 1)
    roll_lo = pltpu.roll(dden - den_hi, HEAD, 1)
    qf, kf, value = qf_i[...], kf_i[...], v_i[...]
    zero = jnp.zeros((TILE, LANES), BF16)
    one = jnp.ones((TILE, LANES), BF16)
    lane = iota((TILE, LANES), 1)
    lane_head = lane // HEAD
    below = iota(square, 0) >= iota(square, 1)
    above = iota(square, 0) <= iota(square, 1)
    prior_hi, prior_lo = split(prior_s[0])
    later_hi, later_lo = split(jnp.where(same, state[...], 0.0))
    d_qf = dot_nt(dn, prior_hi) + dot_nt(dn, prior_lo) + prior_k[0, 0:1, :] * dden
    d_kf = dot_nt(value, later_hi) + dot_nt(value, later_lo) + gsum[0:1, :]
    d_v = dot_nn(kf, later_hi)
    heads = LANES // HEAD
    for h in range(heads):
        here = lane_head == h
        spare = HEAD * ((h + 1) % heads)
        left = jnp.where(lane == spare, roll_hi, jnp.where(lane == spare + 1, roll_lo, dn32)).astype(BF16)
        right = jnp.where(here, value, jnp.where((lane == spare) | (lane == spare + 1), one, zero))
        k_here = jnp.where(here, kf, zero)
        q_here = jnp.where(here, qf, zero)
        d_here = jnp.where(here, dn, zero)
        scores_t = jnp.where(above, dot_nt(k_here, qf), 0.0).astype(BF16)
        ds = jnp.where(below, dot_nt(left, right), 0.0).astype(BF16)
        ds_t = jnp.where(above, dot_nt(right, left), 0.0).astype(BF16)
        d_qf = d_qf + dot_nn(ds, k_here)
        d_kf = d_kf + dot_nn(ds_t, q_here)
        d_v = d_v + dot_nn(scores_t, d_here)
    state[...] = state[...] + dot_tn(qf, dn)
    gsum[...] = gsum[...] + jnp.sum(qf.astype(F32) * dden, axis=0, keepdims=True)
    dlq = d_qf * qf.astype(F32)
    dlk = d_kf * kf.astype(F32)
    fsum[...] = fsum[...] + jnp.sum(dlq + dlk, axis=0, keepdims=True)
    dlq, dlk = dlq.astype(BF16), dlk.astype(BF16)
    dmix[...] = dmix[...] + dot_tn(rq[...], dlq) + dot_tn(rk[...], dlk)
    cosine, sine = twice(cos_t[...]), twice(sin_t[...])
    for c, dl in ((0, dlq), (1, dlk)):
        dr = dot_nt(dl, mix_hi[...])
        dcat[:, c * LANES:(c + 1) * LANES] = (dr * cosine - partner(dr) * sine).astype(BF16)
    dcat[:, 2 * LANES:3 * LANES] = d_v.astype(BF16)
    for c in range(4):
        cols = slice(c * LANES, (c + 1) * LANES)
        d_act = dot_nt(g, w_out[(1 + c) * LANES:(2 + c) * LANES, :])
        dcat[:, (3 + c) * LANES:(4 + c) * LANES] = (d_act * dgelu[:, cols].astype(F32)).astype(BF16)
    wait_weights(step, mine, w_in, w_out, sems, (0, 1, 2, 3))
    wide = dcat[...]
    row = iota((8, LANES), 0)
    first, second = (row == 0).astype(BF16), (row == 1).astype(BF16)
    totals = []

    def product(at):
        part = dot_nt(wide, w_in[at, :])
        one_side = (part * gain[:, at]).astype(BF16)
        other = (part * (normed[:, at].astype(F32) - bias[:, at])).astype(BF16)
        totals.append(dot_nt(first, one_side) + dot_nt(second, other))
        return part

    emit(rank, product, parts)
    stats[...] = totals[0] + totals[1] + totals[2] + totals[3]


def join_kernel(meta, p0, p1, p2, p3a, p3b, whole):
    half = LANES // 2
    for r, piece in enumerate((p0, p1, p2)):
        whole[:, pl.ds(pl.multiple_of((meta[0] ^ r) * LANES, LANES), LANES)] = piece[...]
    at = pl.multiple_of((meta[0] ^ 3) * LANES, LANES)
    whole[:, pl.ds(at, half)] = p3a[...]
    whole[:, pl.ds(pl.multiple_of(at + half, half), half)] = p3b[...]


def partial_outs(rows, phased, row_of):
    half = LANES // 2
    if not phased:
        shapes = [jax.ShapeDtypeStruct((rows, LANES), F32)] + [jax.ShapeDtypeStruct((rows, LANES), BF16)] * 3
        return shapes, [pl.BlockSpec((TILE, LANES), lambda *i: (row_of(*i), 0))] * 4
    shapes = [jax.ShapeDtypeStruct((2, rows, half), BF16)] * 2 + [
        jax.ShapeDtypeStruct((rows, LANES), F32), jax.ShapeDtypeStruct((rows, half), F32),
        jax.ShapeDtypeStruct((rows, half), F32)]
    specs = [pl.BlockSpec((2, TILE, half), lambda *i: (0, row_of(*i), 0))] * 2 + [
        pl.BlockSpec((TILE, width), lambda *i: (row_of(*i), 0)) for width in (LANES, half, half)]
    return shapes, specs


def fixed(shape):
    return pl.BlockSpec(shape, lambda *i: (0,) * len(shape))


def outside(count):
    return [pl.BlockSpec(memory_space=pl.ANY)] * count


def params(axes=1):
    return pltpu.CompilerParams(dimension_semantics=("arbitrary",) * axes, vmem_limit_bytes=56 << 20)


def weight_scratch(width):
    return [pltpu.VMEM((width, 3 * LANES + width), BF16), pltpu.VMEM((LANES + width, width), BF16),
            pltpu.SemaphoreType.DMA((6,))]


def forward_layer(meta, lens, pieces, weights, tables, length, first_row, phased, carry=None):
    rows = pieces[0].shape[0]
    tiles, before = rows // TILE, first_row // TILE
    half, width = LANES // 2, 4 * LANES
    local = lambda t, *_: t
    there = lambda t, *_: before + t
    by_row = lambda n, row_of: pl.BlockSpec((TILE, n), lambda *i: (row_of(*i), 0))
    (gain, bias, mix_hi, mix_lo, feat_w), mine, other = weights
    small = (gain, bias, mix_hi, mix_lo, feat_w)
    shapes, specs = partial_outs(rows, phased, local)
    extra = [(width, BF16), (LANES, F32), (half, F32)] + [(LANES, BF16)] * 5 + [
        (LANES + width, BF16), (width, BF16), (LANES, F32), (LANES, F32)]
    shapes += [jax.ShapeDtypeStruct((length, n), d) for n, d in extra]
    specs += [by_row(n, there) for n, _ in extra]
    shapes += [jax.ShapeDtypeStruct((length // TILE, LANES, LANES), F32), jax.ShapeDtypeStruct((length // TILE, 8, LANES), F32)]
    specs += [pl.BlockSpec((1, n, LANES), lambda *i: (there(*i), 0, 0)) for n in (LANES, 8)]
    states = [(LANES, LANES), (8, LANES)]
    shapes += [jax.ShapeDtypeStruct(s, F32) for s in states]
    specs += [fixed(s) for s in states]
    operands = [meta, jnp.stack([lens[0], jnp.int32(first_row)]), *pieces, *small, *tables, *mine, *other]
    in_specs = [by_row(p.shape[1], local) for p in pieces] + [fixed(w.shape) for w in small] + [by_row(half, there)] * 2 + outside(8)
    aliases = {}
    if carry is not None:
        state, saved = carry
        operands += [*state, *saved]
        in_specs += [fixed(s) for s in states] + outside(SAVED)
        aliases = {len(operands) - SAVED + i: len(shapes) - 2 - SAVED + i for i in range(SAVED)}
    outs = pl.pallas_call(
        functools.partial(forward_kernel, carry is not None, phased),
        name="layer_forward",
        out_shape=shapes,
        grid_spec=pltpu.PrefetchScalarGridSpec(
            num_scalar_prefetch=2, grid=(tiles,), in_specs=in_specs, out_specs=specs, scratch_shapes=weight_scratch(width)),
        input_output_aliases=aliases,
        compiler_params=params(),
        cost_estimate=pl.CostEstimate(flops=rows * 20_000_000, transcendentals=rows * 5000, bytes_accessed=24 << 20),
    )(*operands)
    count = 5 if phased else 4
    return outs[:count], outs[count:count + SAVED], outs[count + SAVED:]


def backward_layer(meta, grad, saved, weights, tables, length, first_row, phased, carry=None):
    rows = grad.shape[0]
    tiles, before = rows // TILE, first_row // TILE
    half, width = LANES // 2, 4 * LANES
    local = lambda t, *_: tiles - 1 - t
    there = lambda t, *_: before + tiles - 1 - t
    by_row = lambda n, row_of=there: pl.BlockSpec((TILE, n), lambda *i: (row_of(*i), 0))
    normed, rq, rk, qf, kf, value, hcat, dgelu, invz, attended, prior_s, prior_k = saved
    (gain, bias, mix_hi, mix_lo, feat_w), mine, other = weights
    shapes, specs = partial_outs(rows, phased, local)
    shapes += [jax.ShapeDtypeStruct((8, length), F32), jax.ShapeDtypeStruct((length, 3 * LANES + width), BF16)]
    specs += [pl.BlockSpec((8, TILE), lambda *i: (0, there(*i))), by_row(3 * LANES + width)]
    states = [(LANES, LANES), (8, LANES)] * 2
    shapes += [jax.ShapeDtypeStruct(s, F32) for s in states]
    specs += [fixed(s) for s in states]
    operands = [meta, grad, normed, rq, rk, qf, kf, value, attended, dgelu, invz, prior_s, prior_k, gain, bias, mix_hi, *tables,
                *mine, *other]
    in_specs = [by_row(width, local), by_row(width)] + [by_row(LANES)] * 6 + [by_row(width), by_row(LANES)] + [
        pl.BlockSpec((1, n, LANES), lambda *i: (there(*i), 0, 0)) for n in (LANES, 8)] + [
        fixed(w.shape) for w in (gain, bias, mix_hi)] + [by_row(half)] * 2 + outside(8)
    aliases = {}
    if carry is not None:
        state, arrays = carry
        operands += [*state, *arrays]
        in_specs += [fixed(s) for s in states] + outside(2)
        aliases = {len(operands) - 2 + i: len(shapes) - 6 + i for i in range(2)}
    outs = pl.pallas_call(
        functools.partial(backward_kernel, carry is not None, phased),
        name="layer_backward",
        out_shape=shapes,
        grid_spec=pltpu.PrefetchScalarGridSpec(
            num_scalar_prefetch=1, grid=(tiles,), in_specs=in_specs, out_specs=specs, scratch_shapes=weight_scratch(width)),
        input_output_aliases=aliases,
        compiler_params=params(),
        cost_estimate=pl.CostEstimate(flops=rows * 25_000_000, transcendentals=0, bytes_accessed=24 << 20),
    )(*operands)
    count = 5 if phased else 4
    return outs[:count], outs[count:count + 2], outs[count + 2:]


def join(meta, pieces):
    rows, block = pieces[0].shape[0], 2 * TILE
    return pl.pallas_call(
        join_kernel,
        name="join",
        out_shape=jax.ShapeDtypeStruct((rows, 4 * LANES), BF16),
        grid_spec=pltpu.PrefetchScalarGridSpec(
            num_scalar_prefetch=1,
            grid=(rows // block,),
            in_specs=[pl.BlockSpec((block, p.shape[1]), lambda i, *_: (i, 0)) for p in pieces],
            out_specs=pl.BlockSpec((block, 4 * LANES), lambda i, *_: (i, 0)),
        ),
        cost_estimate=pl.CostEstimate(flops=0, transcendentals=0, bytes_accessed=rows * 16 * LANES),
    )(meta, *pieces)


def swap(value, axis, by):
    return lax.ppermute(value, axis, [(k, k ^ by) for k in range(lax.axis_size(axis))])


def gather_pieces(shard, meanwhile=()):
    half = shard.shape[1] // 2
    from_x, from_y = after((swap(shard, "mp", 1), swap(shard, "mp", 2)), *meanwhile)
    return shard, from_x, from_y, swap(from_x[:, :half], "mp", 2), swap(from_y[:, half:], "mp", 1)


def after(values, *others):
    if not others:
        return values
    return lax.optimization_barrier((values, others))[0]


def direct_sends(parts):
    return parts[0], [swap(part, "mp", r) for r, part in enumerate(parts) if r > 0]


def scatter_sum(parts, extra, meanwhile=()):
    sx, sy, k0, ka, kb = parts
    half = ka.shape[1]
    in_x, in_y = after((swap(sx, "mp", 1), swap(sy, "mp", 2)), *meanwhile)
    if extra is not None:
        extra = mp_total(after(extra, in_x, in_y))
    last_y = swap((ka + in_x[1].astype(F32)).astype(BF16), "mp", 2)
    last_x = swap((kb + in_y[1].astype(F32)).astype(BF16), "mp", 1)
    return jnp.concatenate(
        [k0[:, :half] + in_x[0].astype(F32) + last_y.astype(F32), k0[:, half:] + in_y[0].astype(F32) + last_x.astype(F32)],
        axis=1), extra


def mp_total(values):
    return values + swap(values, "mp", 1) + swap(values, "mp", 2) + swap(values, "mp", 3)


def ring_scatter(block_of, axis):
    count = lax.axis_size(axis)
    rank = lax.axis_index(axis)
    pairs = [(k, (k + 1) % count) for k in range(count)]
    total = block_of((rank + count - 1) % count)
    for step in range(2, count + 1):
        arrived = lax.ppermute(total, axis, pairs)
        total = (arrived.astype(F32) + block_of((rank + count - step) % count).astype(F32)).astype(BF16)
    return total


def dp_total(values):
    count = lax.axis_size("dp")
    if count > 8:
        return lax.psum(values, "dp")
    sent = [lax.ppermute(values, "dp", [(i, (i + k) % count) for i in range(count)]) for k in range(1, count)]
    return sum(sent, values)


def block_sends(block_of, axis):
    count = lax.axis_size(axis)
    rank = lax.axis_index(axis)
    if count > 8:
        return [ring_scatter(block_of, axis)]
    return [block_of(rank)] + [
        lax.ppermute(block_of((rank + k) % count), axis, [(i, (i + k) % count) for i in range(count)]) for k in range(1, count)]


def sum_blocks(blocks):
    total = blocks[0].astype(F32)
    for block in blocks[1:]:
        total = total + block.astype(F32)
    return total.astype(BF16)


def weight_gradient(left, right, half_of, section):
    def product(which):
        a, b = half_of(left, right, which)
        return lax.dot_general(a, b, (((0,), (0,)), ((), ())), preferred_element_type=F32).astype(BF16)

    arrived = swap(product(1 - section), "section", 1)
    return lax.optimization_barrier(product(section)), arrived


def dct_table(order):
    row_index = jnp.arange(order, dtype=F32)[:, None]
    col_index = jnp.arange(order, dtype=F32)[None, :]
    cosines = jnp.sqrt(2.0 / order) * jnp.cos(math.pi * (row_index + 0.5) * col_index / order)
    return cosines * jnp.where(col_index == 0, math.sqrt(0.5), 1.0)


def rotary_tables(length):
    column = jnp.arange(LANES // 2, dtype=jnp.int32) % HEAD
    half = ROT // 2
    index = (column % half).astype(F32)
    angles = jnp.arange(length, dtype=F32)[:, None] * (10000.0 ** (-index * 2.0 / ROT))[None, :]
    turned = (column < ROT)[None, :]
    sign = jnp.where(column < half, -1.0, 1.0)[None, :]
    return jnp.where(turned, jnp.cos(angles), 1.0), jnp.where(turned, sign * jnp.sin(angles), 0.0)


def shards(block_input, cotangent, lengths, ln_gain, ln_bias, w_qkv, w_out, w_up, w_down, freq_table, feat_weight):
    section = lax.axis_index("section")
    place = lax.axis_index("mp")
    group = lax.axis_index("dp")
    groups = lax.axis_size("dp")
    local_slots, length, shard_width = block_input.shape
    width = ln_gain.shape[1]
    heads = freq_table.shape[1]
    is_first = section == 0
    lens = lax.dynamic_slice_in_dim(lengths, section, 1, 0)
    metas = [jnp.stack([place, (section == l).astype(jnp.int32)]).astype(jnp.int32) for l in range(2)]

    def own(values):
        return lax.dynamic_index_in_dim(values, section, 0, keepdims=False)

    shard0 = own(block_input)
    pieces0 = gather_pieces(shard0)

    small = jnp.concatenate([ln_gain[0], ln_bias[0], feat_weight.reshape(-1), freq_table.astype(F32).reshape(-1)])
    small_other = swap(small, "section", 1)
    mine = (w_qkv, w_up, w_out, w_down)
    other = tuple(swap(w, "section", 1) for w in mine)

    def both(mine, other):
        return jnp.where(is_first, mine, other), jnp.where(is_first, other, mine)

    layers_small = both(small, small_other)
    table = dct_table(HEAD)
    eye = jnp.eye(heads, dtype=F32)

    def layer_weights(l):
        vec = layers_small[l]
        gain, bias = vec[:width].reshape(1, width), vec[width:2 * width].reshape(1, width)
        feat = vec[2 * width:2 * width + LANES].reshape(1, LANES)
        freq = vec[2 * width + LANES:].reshape(heads, HEAD, HEAD)
        mixed = jnp.einsum("nk,hkm->hnm", table, freq, precision=lax.Precision.HIGHEST)
        mixed = (eye[:, None, :, None] * mixed[:, :, None, :]).reshape(LANES, LANES)
        high = lax.reduce_precision(mixed, 8, 7)
        return (gain, bias, high.astype(BF16), (mixed - high).astype(BF16), feat), mine, other

    weights0, weights1 = layer_weights(0), layer_weights(1)
    tables = rotary_tables(length)

    cot = after(own(cotangent), pieces0[3], pieces0[4])
    cot_x, cot_y = swap(cot, "mp", 1), swap(cot, "mp", 2)
    part0, all0, _ = forward_layer(metas[0], lens, pieces0, weights0, tables, length, 0, True)
    part0 = after(part0, cot_x, cot_y)
    hidden = (shard0.astype(F32) + scatter_sum(part0, None)[0]).astype(BF16)
    pieces1 = gather_pieces(hidden)
    cot_x, cot_y = after((cot_x, cot_y), pieces1[3], pieces1[4])
    half = shard_width // 2
    pieces_g = cot, cot_x, cot_y, swap(cot_x[:, :half], "mp", 2), swap(cot_y[:, half:], "mp", 1)
    part1, all1, _ = forward_layer(metas[1], lens, pieces1, weights1, tables, length, 0, False)
    out_kept, out_sent = direct_sends(part1)

    def saved_of(arrays):
        return (arrays[0],) + tuple(arrays[3:])

    def in_half(left, right, which):
        n = right.shape[1] // 2
        return left, lax.dynamic_slice_in_dim(right, which * n, n, 1)

    def out_half(left, right, which):
        n = left.shape[1] // 2
        return lax.dynamic_slice_in_dim(left, which * n, n, 1), right

    def in_block(mine, arrived):
        n = mine.shape[0] // groups
        cut = lambda v, i: lax.dynamic_slice_in_dim(v, i * n, n, 0)
        return lambda i: (cut(mine, i).astype(F32) + cut(arrived, i).astype(F32)).astype(BF16)

    def out_block(mine, arrived):
        n = mine.shape[1] // groups
        cut = lambda v, i: lax.dynamic_slice_in_dim(v, i * n, n, 1)
        return lambda i: (cut(mine, i).astype(F32) + cut(arrived, i).astype(F32)).astype(BF16)

    def run_backward(meta, grad, saved, weights, phased):
        parts, (stats, dcat), (_, _, dmix, fsum) = backward_layer(meta, grad, saved, weights, tables, length, 0, phased)
        return parts, stats, dcat, dmix, fsum

    def norm_backward(grad_shard, d_normed, sums, norm, gain_all):
        xhat, rstd = norm
        gain = lax.dynamic_slice_in_dim(gain_all, place * shard_width, shard_width, 1)
        mean_d = (sums[0] * (1.0 / width))[:, None]
        mean_dx = (sums[1] * (1.0 / width))[:, None]
        return grad_shard.astype(F32) + rstd[:, :1] * (d_normed * gain - mean_d - xhat * mean_dx)

    def small_gradients(d_normed, norm, dmix, fsum):
        gain_part = jnp.sum(d_normed * norm[0], axis=0)
        bias_part = jnp.sum(d_normed, axis=0)
        diagonal = jnp.stack([dmix[h * HEAD:(h + 1) * HEAD, h * HEAD:(h + 1) * HEAD] for h in range(heads)])
        return jnp.concatenate([gain_part, bias_part, fsum[0], diagonal.reshape(-1)])

    saved1, saved0 = saved_of(all1), saved_of(all0)
    grad1 = join(metas[1], pieces_g)
    out_blocks1 = block_sends(out_block(*weight_gradient(saved1[6], grad1, out_half, section)), "dp")
    grad1_b = after(grad1, out_blocks1[0])
    parts, stats, dcat1, dmix1, fsum1 = run_backward(metas[1], grad1_b, saved1, weights1, True)
    parts, stats, dcat1, dmix1, fsum1 = after((parts, stats, dcat1, dmix1, fsum1), *out_blocks1, *out_sent)
    in_blocks1 = block_sends(in_block(*weight_gradient(saved1[0], dcat1, in_half, section)), "dp")
    d_normed, sums = scatter_sum(parts, stats, in_blocks1[:1])
    g0 = norm_backward(cot, d_normed, sums, all1[1:3], weights1[0][0]).astype(BF16)
    small1 = small_gradients(d_normed, all1[1:3], dmix1, fsum1)
    pieces_g0 = after(gather_pieces(g0, in_blocks1[1:2]), *in_blocks1[:3])
    out = hidden.astype(F32) + out_kept + out_sent[0].astype(F32) + out_sent[1].astype(F32) + out_sent[2].astype(F32)

    grad0 = join(metas[0], pieces_g0)
    mine0, arrived0 = after(weight_gradient(saved0[6], grad0, out_half, section), *in_blocks1)
    out_blocks0 = block_sends(out_block(mine0, arrived0), "dp")
    grad0_b = after(grad0, out_blocks0[0])
    parts, stats, dcat0, dmix0, fsum0 = run_backward(metas[0], grad0_b, saved0, weights0, False)
    parts, stats, dcat0, dmix0, fsum0 = after((parts, stats, dcat0, dmix0, fsum0), *out_blocks0)
    out_blocks1, in_blocks1 = after((out_blocks1, in_blocks1), dcat0)
    kept, sent = direct_sends(parts)
    sums = mp_total(stats)
    mine0, arrived0 = weight_gradient(saved0[0], dcat0, in_half, section)
    in_blocks0 = block_sends(in_block(mine0, arrived0), "dp")
    red_in0 = sum_blocks(in_blocks0)
    red_out1, red_in1, red_out0 = sum_blocks(out_blocks1), sum_blocks(in_blocks1), sum_blocks(out_blocks0)
    sent, dmix0 = after((sent, dmix0), *in_blocks0[1::2])
    d_normed = kept + sent[0].astype(F32) + sent[1].astype(F32) + sent[2].astype(F32)
    d_input = norm_backward(g0, d_normed, sums, all0[1:3], weights0[0][0])
    small0 = small_gradients(d_normed, all0[1:3], dmix0, fsum0)

    def to_owner(first, second, axis):
        mine, other = both(first, second)
        arrived = swap(other, "section", 1)
        return jnp.where(is_first, jnp.concatenate([mine, arrived], axis), jnp.concatenate([arrived, mine], axis)).astype(F32)

    grads_in = to_owner(red_in0, red_in1, 1)
    grads_out = to_owner(red_out0, red_out1, 0)
    small_mine, small_send = both(small0, small1)
    small_sum = dp_total(small_mine + swap(small_send, "section", 1))
    feat_grad = small_sum[2 * shard_width:2 * shard_width + LANES].reshape(heads, HEAD) / feat_weight[0]
    freq_grad = jnp.einsum("nk,hnm->hkm", table, small_sum[2 * shard_width + LANES:].reshape(heads, HEAD, HEAD),
                           precision=lax.Precision.HIGHEST)
    keep, send = both(d_input, out)
    arrived = swap(send, "section", 1)
    boundary = jnp.where(is_first, jnp.stack([keep, arrived]), jnp.stack([arrived, keep]))
    qkv_grad = jnp.stack([grads_in[:, t * shard_width:(t + 1) * shard_width] for t in range(3)])
    return (
        boundary[None],
        small_sum[None, :shard_width],
        small_sum[None, shard_width:2 * shard_width],
        qkv_grad[None],
        grads_out[None, :shard_width],
        grads_in[None, :, 3 * shard_width:],
        grads_out[None, shard_width:],
        freq_grad[None],
        feat_grad[None],
    )


def solution(mesh):
    placed = (
        P("dp", None, "mp"), P("dp", None, "mp"), P("dp"), P("section", None), P("section", None),
        P("section", None, None, "mp"), P("section", "mp", None), P("section", None, "mp"), P("section", "mp", None),
        P("section", "mp", None, None), P("section", "mp", None),
    )
    return jax.shard_map(
        shards,
        mesh=mesh,
        in_specs=placed,
        out_specs=(
            P("section", "dp", None, "mp"), P("section", "mp"), P("section", "mp"), P("section", None, "dp", "mp"),
            P("section", "mp", "dp"), P("section", "dp", "mp"), P("section", "mp", "dp"), P("section", "mp", None, None),
            P("section", "mp", None),
        ),
        check_vma=False,
    )
```

profile of v0, /device:TPU:0, one launch (start us, length us, event | category | flops | bytes accessed | tf_op | source)
XLA Modules:
  0.0 401.2 jit_solution(7875834842851380398)
XLA Ops:
  21.7 3.9 collective-permute-done.3.refs_6_
  35.4 22.5 %layer_forward.2 = (bf16[2,1024,128]{2,1,0:T(8,128)(2,1)}, bf16[2,1024,128]{2,1,0:T(8,128)(2,1)}, f32[1024,256]{1,0:T(8,128)}, f32[1024,128]{1,0:T(8,128)}, f32[...) custom-call(s32[2]{0:T(128)} %get-tuple-element.305.refs_0_.meta, ...), custom_call_target="tpu_custom_call" | custom-call | flops 20480000000 | bytes 25165824 | tf_op jit(solution)/shard_map/layer_forward/pallas_call | solution.py:382
  59.2 8.9 %collective-permute-done.11 = bf16[2,1024,128]{2,1,0:T(8,128)(2,1)S(1)} collective-permute-done((bf16[2,1024,128]{2,1,0:T(8,128)(2,1)}, bf16[2,1024,128]{2,1,0:T(8,128)(2,1)S(1)}, u32[]{:S(2)}, u32[]{:S(2)}) %collective-permute-start.11) | collective-permute-done | bytes 524320 | tf_op jit(solution)/shard_map/ppermute | solution.py:453
  72.6 4.1 %collective-permute-done.12 = bf16[1024,128]{1,0:T(8,128)(2,1)S(1)} collective-permute-done((bf16[1024,128]{1,0:T(8,128)(2,1)S(1)}, bf16[1024,128]{1,0:T(8,128)(2,1)S(1)}, u32[]{:S(2)}, u32[]{:S(2)}) %collective-permute-start.12) | collective-permute-done | bytes 262176 | tf_op jit(solution)/shard_map/ppermute | solution.py:453
  76.6 4.0 %collective-permute-done.14 = bf16[1024,128]{1,0:T(8,128)(2,1)S(1)} collective-permute-done((bf16[1024,128]{1,0:T(8,128)(2,1)S(1)}, bf16[1024,128]{1,0:T(8,128)(2,1)S(1)}, u32[]{:S(2)}, u32[]{:S(2)}) %collective-permute-start.14) | collective-permute-done | bytes 262176 | tf_op jit(solution)/shard_map/ppermute | solution.py:453
  82.0 11.0 %collective-permute-done.16.refs_4_ = bf16[1024,256]{1,0:T(8,128)(2,1)S(1)} collective-permute-done((bf16[1024,256]{1,0:T(8,128)(2,1)S(1)}, bf16[1024,256]{1,0:T(8,128)(2,1)S(1)}, u32[]{:S(2)}, u32[]{:S(2)}) %collective-permute-start.16) | collective-permute-done | bytes 524320 | tf_op jit(solution)/shard_map/ppermute | solution.py:453
  97.7 3.7 collective-permute-done.18.refs_6_
  104.0 22.0 %layer_forward.3 = (f32[1024,256]{1,0:T(8,128)}, bf16[1024,256]{1,0:T(8,128)(2,1)}, bf16[1024,256]{1,0:T(8,128)(2,1)}, bf16[1024,256]{1,0:T(8,128)(2,1)}, bf16[1...) custom-call(s32[2]{0:T(128)} %pad_add_fusion.refs_0_.meta, ...), custom_call_target="tpu_custom_call" | custom-call | flops 20480000000 | bytes 25165824 | tf_op jit(solution)/shard_map/layer_forward/pallas_call | solution.py:382
  127.4 3.6 join.2.refs_1_
  131.0 4.8 %convolution_convert_fusion.2 = bf16[640,1024]{1,0:T(8,128)(2,1)} fusion(bf16[1024,1024]{1,0:T(8,128)(2,1)} %join.2.refs_1_, bf16[1024,1280]{1,0:T(8,128)(2,1)} %get-tuple-element.128, s32[]{:T(128)S(6)} %select_n.302), kind=kOutput, calls=%fused_computation.15 | convolution fusion | flops 1342832640 | bytes 4718596 | tf_op jit(solution)/shard_map/dot_general | solution.py:527
  142.9 3.7 collective-permute-start.24
  146.6 4.3 %collective-permute-done.25 = bf16[1024,256]{1,0:T(8,128)(2,1)} collective-permute-done((bf16[1024,256]{1,0:T(8,128)(2,1)}, bf16[1024,256]{1,0:T(8,128)(2,1)}, u32[]{:S(2)}, u32[]{:S(2)}) %collective-permute-start.25) | collective-permute-done | bytes 524320 | tf_op jit(solution)/shard_map/ppermute | solution.py:453
  152.5 26.7 %layer_backward.2 = (bf16[2,1024,128]{2,1,0:T(8,128)(2,1)}, bf16[2,1024,128]{2,1,0:T(8,128)(2,1)}, f32[1024,256]{1,0:T(8,128)}, f32[1024,128]{1,0:T(8,128)}, f32...) custom-call(s32[2]{0:T(128)} %pad_add_fusion.refs_0_.meta, ...), custom_call_target="tpu_custom_call" | custom-call | flops 25600000000 | bytes 25165824 | tf_op jit(solution)/shard_map/layer_backward/pallas_call | solution.py:422
  179.4 5.8 %fusion.11 = bf16[1024,896]{1,0:T(8,128)(2,1)} fusion(bf16[1024,1024]{1,0:T(8,128)(2,1)S(1)} %copy-done.61, bf16[1024,1792]{1,0:T(8,128)(2,1)} %get-tuple-element.156, s32[]{:T(128)S(6)} %select_n.310), kind=kOutput, calls=%fused_computation.10 | convolution fusion | flops 1879965696 | bytes 5767172 | tf_op jit(solution)/shard_map/dot_general | solution.py:527
  188.0 4.5 %fusion.8 = bf16[1024,896]{1,0:T(8,128)(2,1)S(1)} fusion(bf16[1024,1024]{1,0:T(8,128)(2,1)} %get-tuple-element.130.refs_2_, bf16[1024,1792]{1,0:T(8,128)(2,1)} %get-tuple-element.156, s32[]{:T(128)S(6)} %select_n.309), kind=kOutput, calls=%fused_computation.9 | convolution fusion | flops 1879965696 | bytes 5767172 | tf_op jit(solution)/shard_map/dot_general | solution.py:527
  193.8 7.0 %collective-permute-done.28 = bf16[2,1024,128]{2,1,0:T(8,128)(2,1)S(1)} collective-permute-done((bf16[2,1024,128]{2,1,0:T(8,128)(2,1)}, bf16[2,1024,128]{2,1,0:T(8,128)(2,1)S(1)}, u32[]{:S(2)}, u32[]{:S(2)}) %collective-permute-start.28) | collective-permute-done | bytes 524320 | tf_op jit(solution)/shard_map/ppermute | solution.py:453
  208.3 4.0 %collective-permute-done.31 = bf16[1024,128]{1,0:T(8,128)(2,1)S(1)} collective-permute-done((bf16[1024,128]{1,0:T(8,128)(2,1)S(1)}, bf16[1024,128]{1,0:T(8,128)(2,1)S(1)}, u32[]{:S(2)}, u32[]{:S(2)}) %collective-permute-start.31) | collective-permute-done | bytes 262176 | tf_op jit(solution)/shard_map/ppermute | solution.py:453
  218.6 12.6 %collective-permute-done.38 = bf16[256,896]{1,0:T(8,128)(2,1)} collective-permute-done((bf16[256,896]{1,0:T(8,128)(2,1)S(1)}, bf16[256,896]{1,0:T(8,128)(2,1)}, u32[]{:S(2)}, u32[]{:S(2)}) %collective-permute-start.38) | collective-permute-done | bytes 458784 | tf_op jit(solution)/shard_map/ppermute | solution.py:514
  233.2 13.8 %collective-permute-done.41 = bf16[256,896]{1,0:T(8,128)(2,1)} collective-permute-done((bf16[256,896]{1,0:T(8,128)(2,1)S(1)}, bf16[256,896]{1,0:T(8,128)(2,1)}, u32[]{:S(2)}, u32[]{:S(2)}) %collective-permute-start.41) | collective-permute-done | bytes 458784 | tf_op jit(solution)/shard_map/ppermute | solution.py:514
  248.4 15.7 %join.3.refs_1_ = bf16[1024,1024]{1,0:T(8,128)(2,1)} custom-call(s32[2]{0:T(128)} %get-tuple-element.305.refs_0_.meta, bf16[1024,256]{1,0:T(8,128)(2,1)} %copy-done.2, bf16[1024,256]{1,0:T(8,128)(2,1)} %copy-done.16, bf16[1024,256]{1,0:T(8,128)(2,1)} %copy-done.15, bf16[1024,128]{1,0:T(8,128)(2,1)} %copy-done.45, bf16[1024,128]{1,0:T(8,128)(2,1)} %copy-done.44), custom_call_target="tpu_custom_call" | custom-call | bytes 4194304 | tf_op jit(solution)/shard_map/join/pallas_call | solution.py:438
  264.2 3.7 convolution_convert_fusion
  274.3 7.6 %collective-permute-done.43 = bf16[256,896]{1,0:T(8,128)(2,1)S(1)} collective-permute-done((bf16[256,896]{1,0:T(8,128)(2,1)S(1)}, bf16[256,896]{1,0:T(8,128)(2,1)S(1)}, u32[]{:S(2)}, u32[]{:S(2)}) %collective-permute-start.43) | collective-permute-done | bytes 458784 | tf_op jit(solution)/shard_map/ppermute | solution.py:514
  283.4 3.4 collective-permute-start.46
  287.5 26.2 %layer_backward.3 = (f32[1024,256]{1,0:T(8,128)}, bf16[1024,256]{1,0:T(8,128)(2,1)}, bf16[1024,256]{1,0:T(8,128)(2,1)}, bf16[1024,256]{1,0:T(8,128)(2,1)}, f32[8...) custom-call(s32[2]{0:T(128)} %get-tuple-element.305.refs_0_.meta, ...), custom_call_target="tpu_custom_call" | custom-call | flops 25600000000 | bytes 25165824 | tf_op jit(solution)/shard_map/layer_backward/pallas_call | solution.py:422
  313.8 5.4 %fusion.17 = bf16[1024,896]{1,0:T(8,128)(2,1)} fusion(bf16[1024,1024]{1,0:T(8,128)(2,1)S(1)} %copy-done.59, bf16[1024,1792]{1,0:T(8,128)(2,1)} %get-tuple-element.200, s32[]{:T(128)S(6)} %select_n.310), kind=kOutput, calls=%fused_computation.12 | convolution fusion | flops 1879965696 | bytes 5767172 | tf_op jit(solution)/shard_map/dot_general | solution.py:527
  324.9 4.0 %fusion.14 = bf16[1024,896]{1,0:T(8,128)(2,1)S(1)} fusion(bf16[1024,1024]{1,0:T(8,128)(2,1)S(1)} %copy-done.60, bf16[1024,1792]{1,0:T(8,128)(2,1)} %get-tuple-element.200, s32[]{:T(128)S(6)} %select_n.309), kind=kOutput, calls=%fused_computation.11 | convolution fusion | flops 1879965696 | bytes 5767172 | tf_op jit(solution)/shard_map/dot_general | solution.py:527
  339.9 4.7 %collective-permute-done.47 = bf16[1024,256]{1,0:T(8,128)(2,1)S(1)} collective-permute-done((bf16[1024,256]{1,0:T(8,128)(2,1)S(1)}, bf16[1024,256]{1,0:T(8,128)(2,1)S(1)}, u32[]{:S(2)}, u32[]{:S(2)}) %collective-permute-start.47) | collective-permute-done | bytes 524320 | tf_op jit(solution)/shard_map/ppermute | solution.py:453
  344.6 3.4 collective-permute-start.61
  347.9 7.0 %collective-permute-done.48 = bf16[1024,256]{1,0:T(8,128)(2,1)S(1)} collective-permute-done((bf16[1024,256]{1,0:T(8,128)(2,1)S(1)}, bf16[1024,256]{1,0:T(8,128)(2,1)S(1)}, u32[]{:S(2)}, u32[]{:S(2)}) %collective-permute-start.48) | collective-permute-done | bytes 524320 | tf_op jit(solution)/shard_map/ppermute | solution.py:453
  356.1 5.0 %collective-permute-done.51 = bf16[256,896]{1,0:T(8,128)(2,1)S(1)} collective-permute-done((bf16[256,896]{1,0:T(8,128)(2,1)S(1)}, bf16[256,896]{1,0:T(8,128)(2,1)S(1)}, u32[]{:S(2)}, u32[]{:S(2)}) %collective-permute-start.51) | collective-permute-done | bytes 458784 | tf_op jit(solution)/shard_map/ppermute | solution.py:514
  363.1 15.7 %collective-permute-done.61 = bf16[256,896]{1,0:T(8,128)(2,1)} collective-permute-done((bf16[256,896]{1,0:T(8,128)(2,1)}, bf16[256,896]{1,0:T(8,128)(2,1)}, u32[]{:S(2)}, u32[]{:S(2)}) %collective-permute-start.61) | collective-permute-done | bytes 458784 | tf_op jit(solution)/shard_map/ppermute | solution.py:514
  389.1 3.9 collective-permute-done.59
  (324 shorter events, 122.7 us)
Async XLA Ops:
  1.9 15.1 %collective-permute-start.2 = (bf16[1024,256]{1,0:T(8,128)(2,1)S(1)}, bf16[1024,256]{1,0:T(8,128)(2,1)}, u32[]{:S(2)}, u32[]{:S(2)}) collective-permute-start(bf16[1024,256]{1,0:T(8,128)(2,1)S(1)} %dynamic-slice_bitcast_fusion.refs_2_), channel_id=1, source_target_pairs={{0,2},{1,3},{2,0},{3,1},{4,6},{5,7},{6,4},{7,5},{8,10},{9,11},{10,... | collective-permute-start | bytes 1572872 | tf_op jit(solution)/shard_map/ppermute | solution.py:453
  4.9 15.5 %collective-permute-start = (bf16[1024,256]{1,0:T(8,128)(2,1)S(1)}, bf16[1024,256]{1,0:T(8,128)(2,1)}, u32[]{:S(2)}, u32[]{:S(2)}) collective-permute-start(bf16[1024,256]{1,0:T(8,128)(2,1)S(1)} %dynamic-slice_bitcast_fusion.refs_2_), channel_id=1, source_target_pairs={{0,1},{1,0},{2,3},{3,2},{4,5},{5,4},{6,7},{7,6},{8,9},{9,8},{10,11... | collective-permute-start | bytes 1572872 | tf_op jit(solution)/shard_map/ppermute | solution.py:453
  8.9 26.5 %collective-permute-start.6 = (bf16[1,1024,1024]{2,1,0:T(8,128)(2,1)}, bf16[1,1024,1024]{2,1,0:T(8,128)(2,1)}, u32[]{:S(2)}, u32[]{:S(2)}) collective-permute-start(bf16[1,1024,1024]{2,1,0:T(8,128)(2,1)} %refs_19_.3), channel_id=1, source_target_pairs={{0,16},{16,0},{1,17},{17,1},{2,18},{18,2},{3,19},{19,3},{4,20},{20... | collective-permute-start | bytes 6291464 | tf_op jit(solution)/shard_map/ppermute | solution.py:453
  9.4 26.0 %collective-permute-start.8 = (bf16[1,1024,1024]{2,1,0:T(8,128)(2,1)}, bf16[1,1024,1024]{2,1,0:T(8,128)(2,1)}, u32[]{:S(2)}, u32[]{:S(2)}) collective-permute-start(bf16[1,1024,1024]{2,1,0:T(8,128)(2,1)} %refs_21_.3), channel_id=1, source_target_pairs={{0,16},{16,0},{1,17},{17,1},{2,18},{18,2},{3,19},{19,3},{4,20},{20... | collective-permute-start | bytes 6291464 | tf_op jit(solution)/shard_map/ppermute | solution.py:453
  15.0 20.4 %collective-permute-start.5 = (bf16[1,3,1024,256]{3,2,1,0:T(8,128)(2,1)}, bf16[1,3,1024,256]{3,2,1,0:T(8,128)(2,1)}, u32[]{:S(2)}, u32[]{:S(2)}) collective-permute-start(bf16[1,3,1024,256]{3,2,1,0:T(8,128)(2,1)} %refs_18_.3), channel_id=1, source_target_pairs={{0,16},{16,0},{1,17},{17,1},{2,18},{18,2},{3,19},{19,3},{4,20},{20... | collective-permute-start | bytes 4718600 | tf_op jit(solution)/shard_map/ppermute | solution.py:453
  32.3 25.6 %collective-permute-start.10 = (bf16[1024,256]{1,0:T(8,128)(2,1)S(1)}, bf16[1024,256]{1,0:T(8,128)(2,1)S(1)}, u32[]{:S(2)}, u32[]{:S(2)}) collective-permute-start(bf16[1024,256]{1,0:T(8,128)(2,1)S(1)} %dynamic-slice_bitcast_fusion.1.p0), channel_id=1, source_target_pairs={{0,2},{1,3},{2,0},{3,1},{4,6},{5,7},{6,4},{7,5},{8,10},{9,11},{10,... | collective-permute-start | bytes 1572872 | tf_op jit(solution)/shard_map/ppermute | solution.py:453
  33.8 24.1 %collective-permute-start.9 = (bf16[1024,256]{1,0:T(8,128)(2,1)S(1)}, bf16[1024,256]{1,0:T(8,128)(2,1)S(1)}, u32[]{:S(2)}, u32[]{:S(2)}) collective-permute-start(bf16[1024,256]{1,0:T(8,128)(2,1)S(1)} %dynamic-slice_bitcast_fusion.1.p0), channel_id=1, source_target_pairs={{0,1},{1,0},{2,3},{3,2},{4,5},{5,4},{6,7},{7,6},{8,9},{9,8},{10,11... | collective-permute-start | bytes 1572872 | tf_op jit(solution)/shard_map/ppermute | solution.py:453
  101.7 24.3 %collective-permute-start.20 = (bf16[1024,128]{1,0:T(8,128)(2,1)S(1)}, bf16[1024,128]{1,0:T(8,128)(2,1)S(1)}, u32[]{:S(2)}, u32[]{:S(2)}) collective-permute-start(bf16[1024,128]{1,0:T(8,128)(2,1)S(1)} %slice.192), channel_id=1, source_target_pairs={{0,1},{1,0},{2,3},{3,2},{4,5},{5,4},{6,7},{7,6},{8,9},{9,8},{10,11... | collective-permute-start | bytes 786440 | tf_op jit(solution)/shard_map/ppermute | solution.py:453
  103.2 22.8 %collective-permute-start.19 = (bf16[1024,128]{1,0:T(8,128)(2,1)S(1)}, bf16[1024,128]{1,0:T(8,128)(2,1)S(1)}, u32[]{:S(2)}, u32[]{:S(2)}) collective-permute-start(bf16[1024,128]{1,0:T(8,128)(2,1)S(1)} %slice.191), channel_id=1, source_target_pairs={{0,2},{1,3},{2,0},{3,1},{4,6},{5,7},{6,4},{7,5},{8,10},{9,11},{10,... | collective-permute-start | bytes 786440 | tf_op jit(solution)/shard_map/ppermute | solution.py:453
  135.8 15.1 %collective-permute-start.25 = (bf16[1024,256]{1,0:T(8,128)(2,1)}, bf16[1024,256]{1,0:T(8,128)(2,1)}, u32[]{:S(2)}, u32[]{:S(2)}) collective-permute-start(bf16[1024,256]{1,0:T(8,128)(2,1)} %get-tuple-element.150), channel_id=1, source_target_pairs={{0,1},{1,0},{2,3},{3,2},{4,5},{5,4},{6,7},{7,6},{8,9},{9,8},{10,11... | collective-permute-start | bytes 1572872 | tf_op jit(solution)/shard_map/ppermute | solution.py:453
  136.2 43.1 %collective-permute-start.26 = (bf16[1024,256]{1,0:T(8,128)(2,1)}, bf16[1024,256]{1,0:T(8,128)(2,1)S(1)}, u32[]{:S(2)}, u32[]{:S(2)}) collective-permute-start(bf16[1024,256]{1,0:T(8,128)(2,1)} %get-tuple-element.151), channel_id=1, source_target_pairs={{0,2},{1,3},{2,0},{3,1},{4,6},{5,7},{6,4},{7,5},{8,10},{9,11},{10,... | collective-permute-start | bytes 1572872 | tf_op jit(solution)/shard_map/ppermute | solution.py:453
  137.6 41.6 %collective-permute-start.27 = (bf16[1024,256]{1,0:T(8,128)(2,1)}, bf16[1024,256]{1,0:T(8,128)(2,1)S(1)}, u32[]{:S(2)}, u32[]{:S(2)}) collective-permute-start(bf16[1024,256]{1,0:T(8,128)(2,1)} %get-tuple-element.152), channel_id=1, source_target_pairs={{0,3},{1,2},{2,1},{3,0},{4,7},{5,6},{6,5},{7,4},{8,11},{9,10},{10,... | collective-permute-start | bytes 1572872 | tf_op jit(solution)/shard_map/ppermute | solution.py:453
  142.9 36.4 %collective-permute-start.24 = (bf16[640,256]{1,0:T(8,128)(2,1)S(1)}, bf16[640,256]{1,0:T(8,128)(2,1)S(1)}, u32[]{:S(2)}, u32[]{:S(2)}) collective-permute-start(bf16[640,256]{1,0:T(8,128)(2,1)S(1)} %get-tuple-element.261), channel_id=1, source_target_pairs={{0,12},{4,0},{8,4},{12,8},{1,13},{5,1},{9,5},{13,9},{2,14},{6,2},{... | collective-permute-start | bytes 983048 | tf_op jit(solution)/shard_map/ppermute | solution.py:514
  146.6 32.8 %collective-permute-start.23 = (bf16[640,256]{1,0:T(8,128)(2,1)S(1)}, bf16[640,256]{1,0:T(8,128)(2,1)S(1)}, u32[]{:S(2)}, u32[]{:S(2)}) collective-permute-start(bf16[640,256]{1,0:T(8,128)(2,1)S(1)} %get-tuple-element.262), channel_id=1, source_target_pairs={{0,8},{4,12},{8,0},{12,4},{1,9},{5,13},{9,1},{13,5},{2,10},{6,14},... | collective-permute-start | bytes 983048 | tf_op jit(solution)/shard_map/ppermute | solution.py:514
  150.9 28.4 %collective-permute-start.22 = (bf16[640,256]{1,0:T(8,128)(2,1)S(1)}, bf16[640,256]{1,0:T(8,128)(2,1)S(1)}, u32[]{:S(2)}, u32[]{:S(2)}) collective-permute-start(bf16[640,256]{1,0:T(8,128)(2,1)S(1)} %get-tuple-element.263), channel_id=1, source_target_pairs={{0,4},{4,8},{8,12},{12,0},{1,5},{5,9},{9,13},{13,1},{2,6},{6,10},{... | collective-permute-start | bytes 983048 | tf_op jit(solution)/shard_map/ppermute | solution.py:514
  213.6 17.6 %collective-permute-start.37 = (bf16[1024,256]{1,0:T(8,128)(2,1)S(1)}, bf16[1024,256]{1,0:T(8,128)(2,1)S(1)}, u32[]{:S(2)}, u32[]{:S(2)}) collective-permute-start(bf16[1024,256]{1,0:T(8,128)(2,1)S(1)} %get-tuple-element.167.p0), channel_id=1, source_target_pairs={{0,2},{1,3},{2,0},{3,1},{4,6},{5,7},{6,4},{7,5},{8,10},{9,11},{10,... | collective-permute-start | bytes 1572872 | tf_op jit(solution)/shard_map/ppermute | solution.py:453
  214.8 16.4 %collective-permute-start.36 = (bf16[1024,256]{1,0:T(8,128)(2,1)S(1)}, bf16[1024,256]{1,0:T(8,128)(2,1)S(1)}, u32[]{:S(2)}, u32[]{:S(2)}) collective-permute-start(bf16[1024,256]{1,0:T(8,128)(2,1)S(1)} %get-tuple-element.167.p0), channel_id=1, source_target_pairs={{0,1},{1,0},{2,3},{3,2},{4,5},{5,4},{6,7},{7,6},{8,9},{9,8},{10,11... | collective-permute-start | bytes 1572872 | tf_op jit(solution)/shard_map/ppermute | solution.py:453
  215.9 15.3 %collective-permute-start.38 = (bf16[256,896]{1,0:T(8,128)(2,1)S(1)}, bf16[256,896]{1,0:T(8,128)(2,1)}, u32[]{:S(2)}, u32[]{:S(2)}) collective-permute-start(bf16[256,896]{1,0:T(8,128)(2,1)S(1)} %get-tuple-element.255), channel_id=1, source_target_pairs={{0,4},{4,8},{8,12},{12,0},{1,5},{5,9},{9,13},{13,1},{2,6},{6,10},{... | collective-permute-start | bytes 1376264 | tf_op jit(solution)/shard_map/ppermute | solution.py:514
  217.4 29.6 %collective-permute-start.41 = (bf16[256,896]{1,0:T(8,128)(2,1)S(1)}, bf16[256,896]{1,0:T(8,128)(2,1)}, u32[]{:S(2)}, u32[]{:S(2)}) collective-permute-start(bf16[256,896]{1,0:T(8,128)(2,1)S(1)} %get-tuple-element.254), channel_id=1, source_target_pairs={{0,8},{4,12},{8,0},{12,4},{1,9},{5,13},{9,1},{13,5},{2,10},{6,14},... | collective-permute-start | bytes 1376264 | tf_op jit(solution)/shard_map/ppermute | solution.py:514
  231.3 15.7 %collective-permute-start.40 = (bf16[1024,128]{1,0:T(8,128)(2,1)S(1)}, bf16[1024,128]{1,0:T(8,128)(2,1)S(1)}, u32[]{:S(2)}, u32[]{:S(2)}) collective-permute-start(bf16[1024,128]{1,0:T(8,128)(2,1)S(1)} %slice.203), channel_id=1, source_target_pairs={{0,1},{1,0},{2,3},{3,2},{4,5},{5,4},{6,7},{7,6},{8,9},{9,8},{10,11... | collective-permute-start | bytes 786440 | tf_op jit(solution)/shard_map/ppermute | solution.py:453
  232.3 14.7 %collective-permute-start.39 = (bf16[1024,128]{1,0:T(8,128)(2,1)S(1)}, bf16[1024,128]{1,0:T(8,128)(2,1)S(1)}, u32[]{:S(2)}, u32[]{:S(2)}) collective-permute-start(bf16[1024,128]{1,0:T(8,128)(2,1)S(1)} %slice.202), channel_id=1, source_target_pairs={{0,2},{1,3},{2,0},{3,1},{4,6},{5,7},{6,4},{7,5},{8,10},{9,11},{10,... | collective-permute-start | bytes 786440 | tf_op jit(solution)/shard_map/ppermute | solution.py:453
  267.9 14.8 %collective-permute-start.42 = (bf16[640,1024]{1,0:T(8,128)(2,1)S(1)}, bf16[640,1024]{1,0:T(8,128)(2,1)S(1)}, u32[]{:S(2)}, u32[]{:S(2)}) collective-permute-start(bf16[640,1024]{1,0:T(8,128)(2,1)S(1)} %convolution_convert_fusion), channel_id=1, source_target_pairs={{0,16},{16,0},{1,17},{17,1},{2,18},{18,2},{3,19},{19,3},{4,20},{20... | collective-permute-start | bytes 3932168 | tf_op jit(solution)/shard_map/ppermute | solution.py:453
  283.4 30.3 %collective-permute-start.46 = (bf16[640,256]{1,0:T(8,128)(2,1)S(1)}, bf16[640,256]{1,0:T(8,128)(2,1)S(1)}, u32[]{:S(2)}, u32[]{:S(2)}) collective-permute-start(bf16[640,256]{1,0:T(8,128)(2,1)S(1)} %get-tuple-element.257), channel_id=1, source_target_pairs={{0,12},{4,0},{8,4},{12,8},{1,13},{5,1},{9,5},{13,9},{2,14},{6,2},{... | collective-permute-start | bytes 983048 | tf_op jit(solution)/shard_map/ppermute | solution.py:514
  286.9 27.0 %collective-permute-start.45 = (bf16[640,256]{1,0:T(8,128)(2,1)S(1)}, bf16[640,256]{1,0:T(8,128)(2,1)S(1)}, u32[]{:S(2)}, u32[]{:S(2)}) collective-permute-start(bf16[640,256]{1,0:T(8,128)(2,1)S(1)} %get-tuple-element.258), channel_id=1, source_target_pairs={{0,8},{4,12},{8,0},{12,4},{1,9},{5,13},{9,1},{13,5},{2,10},{6,14},... | collective-permute-start | bytes 983048 | tf_op jit(solution)/shard_map/ppermute | solution.py:514
  286.9 27.0 %collective-permute-start.44 = (bf16[640,256]{1,0:T(8,128)(2,1)S(1)}, bf16[640,256]{1,0:T(8,128)(2,1)S(1)}, u32[]{:S(2)}, u32[]{:S(2)}) collective-permute-start(bf16[640,256]{1,0:T(8,128)(2,1)S(1)} %get-tuple-element.259), channel_id=1, source_target_pairs={{0,4},{4,8},{8,12},{12,0},{1,5},{5,9},{9,13},{13,1},{2,6},{6,10},{... | collective-permute-start | bytes 983048 | tf_op jit(solution)/shard_map/ppermute | solution.py:514
  329.7 14.9 %collective-permute-start.47 = (bf16[1024,256]{1,0:T(8,128)(2,1)S(1)}, bf16[1024,256]{1,0:T(8,128)(2,1)S(1)}, u32[]{:S(2)}, u32[]{:S(2)}) collective-permute-start(bf16[1024,256]{1,0:T(8,128)(2,1)S(1)} %copy-done.57), channel_id=1, source_target_pairs={{0,1},{1,0},{2,3},{3,2},{4,5},{5,4},{6,7},{7,6},{8,9},{9,8},{10,11... | collective-permute-start | bytes 1572872 | tf_op jit(solution)/shard_map/ppermute | solution.py:453
  330.8 24.1 %collective-permute-start.48 = (bf16[1024,256]{1,0:T(8,128)(2,1)S(1)}, bf16[1024,256]{1,0:T(8,128)(2,1)S(1)}, u32[]{:S(2)}, u32[]{:S(2)}) collective-permute-start(bf16[1024,256]{1,0:T(8,128)(2,1)S(1)} %copy-done.56), channel_id=1, source_target_pairs={{0,2},{1,3},{2,0},{3,1},{4,6},{5,7},{6,4},{7,5},{8,10},{9,11},{10,... | collective-permute-start | bytes 1572872 | tf_op jit(solution)/shard_map/ppermute | solution.py:453
  332.1 23.9 %collective-permute-start.49 = (bf16[1024,256]{1,0:T(8,128)(2,1)S(1)}, bf16[1024,256]{1,0:T(8,128)(2,1)S(1)}, u32[]{:S(2)}, u32[]{:S(2)}) collective-permute-start(bf16[1024,256]{1,0:T(8,128)(2,1)S(1)} %copy-done.55), channel_id=1, source_target_pairs={{0,3},{1,2},{2,1},{3,0},{4,7},{5,6},{6,5},{7,4},{8,11},{9,10},{10,... | collective-permute-start | bytes 1572872 | tf_op jit(solution)/shard_map/ppermute | solution.py:453
  334.9 21.1 %collective-permute-start.52 = (bf16[256,896]{1,0:T(8,128)(2,1)S(1)}, bf16[256,896]{1,0:T(8,128)(2,1)S(1)}, u32[]{:S(2)}, u32[]{:S(2)}) collective-permute-start(bf16[256,896]{1,0:T(8,128)(2,1)S(1)} %get-tuple-element.251), channel_id=1, source_target_pairs={{0,12},{4,0},{8,4},{12,8},{1,13},{5,1},{9,5},{13,9},{2,14},{6,2},{... | collective-permute-start | bytes 1376264 | tf_op jit(solution)/shard_map/ppermute | solution.py:514
  338.1 22.9 %collective-permute-start.51 = (bf16[256,896]{1,0:T(8,128)(2,1)S(1)}, bf16[256,896]{1,0:T(8,128)(2,1)S(1)}, u32[]{:S(2)}, u32[]{:S(2)}) collective-permute-start(bf16[256,896]{1,0:T(8,128)(2,1)S(1)} %get-tuple-element.252), channel_id=1, source_target_pairs={{0,4},{4,8},{8,12},{12,0},{1,5},{5,9},{9,13},{13,1},{2,6},{6,10},{... | collective-permute-start | bytes 1376264 | tf_op jit(solution)/shard_map/ppermute | solution.py:514
  344.6 34.2 %collective-permute-start.61 = (bf16[256,896]{1,0:T(8,128)(2,1)}, bf16[256,896]{1,0:T(8,128)(2,1)}, u32[]{:S(2)}, u32[]{:S(2)}) collective-permute-start(bf16[256,896]{1,0:T(8,128)(2,1)} %get-tuple-element.250), channel_id=1, source_target_pairs={{0,8},{4,12},{8,0},{12,4},{1,9},{5,13},{9,1},{13,5},{2,10},{6,14},... | collective-permute-start | bytes 1376264 | tf_op jit(solution)/shard_map/ppermute | solution.py:514
  363.0 19.9 %collective-permute-start.57 = (f32[17152]{0:T(1024)S(1)}, f32[17152]{0:T(1024)S(1)}, u32[]{:S(2)}, u32[]{:S(2)}) collective-permute-start(f32[17152]{0:T(1024)S(1)} %fusion.38), channel_id=1, source_target_pairs={{0,16},{16,0},{1,17},{17,1},{2,18},{18,2},{3,19},{19,3},{4,20},{20... | collective-permute-start | bytes 205832 | tf_op jit(solution)/shard_map/ppermute | solution.py:453
  (94 other events, 1051.3 us)
where the time goes:
time: 405 us; the launch traced here: 401 us
  waiting for transfers between devices  129 us (32%)
  Pallas kernels  117 us (29%)
  starting transfers between devices  66.2 us (16%)
  matrix products  35.3 us (9%)
  other arithmetic  28.6 us (7%)
  local copies, waits for them, and re-layouts  23.6 us (6%)
    ppermute x49, waiting for transfers between devices, swap(): lax.ppermute(value, axis, [(k, k ^ by) for k in range(lax.axis_size(axis))])  70.2 us
    ppermute x12, waiting for transfers between devices, block_sends(): lax.ppermute(block_of((rank + k) % count), axis, [(i, (i + k) % count) fo...  54.8 us
    pallas_call x2, Pallas kernels, backward_layer(): pl.pallas_call(functools.partial(backward_kernel, carry is not None, phas...  52.9 us
    pallas_call x2, Pallas kernels, forward_layer(): pl.pallas_call(functools.partial(forward_kernel, carry is not None, phase...  44.4 us
    ppermute x49, starting transfers between devices, swap(): lax.ppermute(value, axis, [(k, k ^ by) for k in range(lax.axis_size(axis))])  42.5 us
    dot_general x8, matrix products, product(): lax.dot_general(a, b, (((0,), (0,)), ((), ())), preferred_element_type=F32)  33.9 us
    ppermute x12, starting transfers between devices, block_sends(): lax.ppermute(block_of((rank + k) % count), axis, [(i, (i + k) % count) fo...  20.4 us
    pallas_call x2, Pallas kernels, join(): pl.pallas_call(join_kernel, name='join', out_shape=jax.ShapeDtypeStruct((...  19.3 us
  transfers between devices with their start and end apart: 64, of which 26 were waited for; matrix products, arithmetic and copies ran while one was open for 14% of the time, Pallas kernels for 24%

commit v1 on v0

--- a/solution.py
+++ b/solution.py
@@ -469,17 +469,29 @@
     return parts[0], [swap(part, "mp", r) for r, part in enumerate(parts) if r > 0]
 
 
-def scatter_sum(parts, extra, meanwhile=()):
-    sx, sy, k0, ka, kb = parts
+def scatter_start(parts):
+    return swap(parts[0], "mp", 1), swap(parts[1], "mp", 2)
+
+
+def scatter_turn(parts, arrived):
+    _, _, _, ka, kb = parts
+    in_x, in_y = arrived
+    return (ka + in_x[1].astype(F32)).astype(BF16), (kb + in_y[1].astype(F32)).astype(BF16)
+
+
+def scatter_end(parts, arrived, to_y, to_x):
+    _, _, k0, ka, _ = parts
+    in_x, in_y = arrived
     half = ka.shape[1]
-    in_x, in_y = after((swap(sx, "mp", 1), swap(sy, "mp", 2)), *meanwhile)
-    if extra is not None:
-        extra = mp_total(after(extra, in_x, in_y))
-    last_y = swap((ka + in_x[1].astype(F32)).astype(BF16), "mp", 2)
-    last_x = swap((kb + in_y[1].astype(F32)).astype(BF16), "mp", 1)
+    last_y, last_x = swap(to_y, "mp", 2), swap(to_x, "mp", 1)
     return jnp.concatenate(
         [k0[:, :half] + in_x[0].astype(F32) + last_y.astype(F32), k0[:, half:] + in_y[0].astype(F32) + last_x.astype(F32)],
-        axis=1), extra
+        axis=1)
+
+
+def scatter_sum(parts):
+    arrived = scatter_start(parts)
+    return scatter_end(parts, arrived, *scatter_turn(parts, arrived))
 
 
 def mp_total(values):
@@ -521,13 +533,13 @@
     return total.astype(BF16)
 
 
-def weight_gradient(left, right, half_of, section):
-    def product(which):
-        a, b = half_of(left, right, which)
+def weight_gradient(left, right, half_of, section, *before_own):
+    def product(which, *before):
+        a, b = half_of(left, after(right, *before), which)
         return lax.dot_general(a, b, (((0,), (0,)), ((), ())), preferred_element_type=F32).astype(BF16)
 
     arrived = swap(product(1 - section), "section", 1)
-    return lax.optimization_barrier(product(section)), arrived
+    return lax.optimization_barrier(product(section, *before_own)), arrived
 
 
 def dct_table(order):
@@ -594,7 +606,7 @@
     cot_x, cot_y = swap(cot, "mp", 1), swap(cot, "mp", 2)
     part0, all0, _ = forward_layer(metas[0], lens, pieces0, weights0, tables, length, 0, True)
     part0 = after(part0, cot_x, cot_y)
-    hidden = (shard0.astype(F32) + scatter_sum(part0, None)[0]).astype(BF16)
+    hidden = (shard0.astype(F32) + scatter_sum(part0)).astype(BF16)
     pieces1 = gather_pieces(hidden)
     cot_x, cot_y = after((cot_x, cot_y), pieces1[3], pieces1[4])
     half = shard_width // 2
@@ -646,11 +658,15 @@
     grad1_b = after(grad1, out_blocks1[0])
     parts, stats, dcat1, dmix1, fsum1 = run_backward(metas[1], grad1_b, saved1, weights1, True)
     parts, stats, dcat1, dmix1, fsum1 = after((parts, stats, dcat1, dmix1, fsum1), *out_blocks1, *out_sent)
+    arrived = scatter_start(parts)
+    turn = scatter_turn(parts, arrived)
+    sums = mp_total(after(stats, *turn))
+    dcat1 = after(dcat1, *turn)
     in_blocks1 = block_sends(in_block(*weight_gradient(saved1[0], dcat1, in_half, section)), "dp")
-    d_normed, sums = scatter_sum(parts, stats, in_blocks1[:1])
+    d_normed = scatter_end(parts, arrived, *turn)
     g0 = norm_backward(cot, d_normed, sums, all1[1:3], weights1[0][0]).astype(BF16)
     small1 = small_gradients(d_normed, all1[1:3], dmix1, fsum1)
-    pieces_g0 = after(gather_pieces(g0, in_blocks1[1:2]), *in_blocks1[:3])
+    pieces_g0 = after(gather_pieces(after(g0, *in_blocks1[:2])), *in_blocks1[:3])
     out = hidden.astype(F32) + out_kept + out_sent[0].astype(F32) + out_sent[1].astype(F32) + out_sent[2].astype(F32)
 
     grad0 = join(metas[0], pieces_g0)
@@ -664,9 +680,7 @@
     sums = mp_total(stats)
     mine0, arrived0 = weight_gradient(saved0[0], dcat0, in_half, section)
     in_blocks0 = block_sends(in_block(mine0, arrived0), "dp")
-    red_in0 = sum_blocks(in_blocks0)
-    red_out1, red_in1, red_out0 = sum_blocks(out_blocks1), sum_blocks(in_blocks1), sum_blocks(out_blocks0)
-    sent, dmix0 = after((sent, dmix0), *in_blocks0[1::2])
+    sent, dmix0, out_blocks0, out_blocks1, in_blocks1 = after((sent, dmix0, out_blocks0, out_blocks1, in_blocks1), *in_blocks0[:2])
     d_normed = kept + sent[0].astype(F32) + sent[1].astype(F32) + sent[2].astype(F32)
     d_input = norm_backward(g0, d_normed, sums, all0[1:3], weights0[0][0])
     small0 = small_gradients(d_normed, all0[1:3], dmix0, fsum0)
@@ -676,8 +690,8 @@
         arrived = swap(other, "section", 1)
         return jnp.where(is_first, jnp.concatenate([mine, arrived], axis), jnp.concatenate([arrived, mine], axis)).astype(F32)
 
-    grads_in = to_owner(red_in0, red_in1, 1)
-    grads_out = to_owner(red_out0, red_out1, 0)
+    grads_out = to_owner(sum_blocks(out_blocks0), sum_blocks(out_blocks1), 0)
+    red_in1 = sum_blocks(in_blocks1)
     small_mine, small_send = both(small0, small1)
     small_sum = dp_total(small_mine + swap(small_send, "section", 1))
     feat_grad = small_sum[2 * shard_width:2 * shard_width + LANES].reshape(heads, HEAD) / feat_weight[0]
@@ -686,6 +700,8 @@
     keep, send = both(d_input, out)
     arrived = swap(send, "section", 1)
     boundary = jnp.where(is_first, jnp.stack([keep, arrived]), jnp.stack([arrived, keep]))
+    in_blocks0 = after(in_blocks0, grads_out, small_sum, boundary, red_in1)
+    grads_in = to_owner(sum_blocks(in_blocks0), red_in1, 1)
     qkv_grad = jnp.stack([grads_in[:, t * shard_width:(t + 1) * shard_width] for t in range(3)])
     return (
         boundary[None],

time: 405 us -> 399 us (0.985)
  waiting for transfers between devices: 129 us -> 107 us
  starting transfers between devices: 66.2 us -> 85.7 us
  matrix products: 35.3 us -> 31.2 us
    ppermute x12, waiting for transfers between devices: 54.8 us -> 25.7 us  [block_sends(): lax.ppermute(block_of((rank + k) % count), axis, [(i, (i + k) % count) fo...]
    ppermute x3, starting transfers between devices: 3.34 us -> 20 us  [dp_total(): lax.ppermute(values, 'dp', [(i, (i + k) % count) for i in range(count)])]
    ppermute x49, waiting for transfers between devices: 70.2 us -> 77.5 us  [swap(): lax.ppermute(value, axis, [(k, k ^ by) for k in range(lax.axis_size(axis))])]
    dot_general x8, matrix products: 33.9 us -> 29.9 us  [product(): lax.dot_general(a, b, (((0,), (0,)), ((), ())), preferred_element_type=F32)]
  transfers between devices with their start and end apart: 64 -> 64, of which waited for: 26 -> 20; matrix products, arithmetic and copies ran while one was open for 14% -> 14% of each run, Pallas kernels for 24% -> 25%
where the time goes in v1:
time: 399 us; the launch traced here: 395 us
  Pallas kernels  117 us (29%)
  waiting for transfers between devices  107 us (27%)
  starting transfers between devices  85.7 us (21%)
  other arithmetic  32 us (8%)
  matrix products  31.2 us (8%)
  local copies, waits for them, and re-layouts  20.3 us (5%)
    ppermute x49, waiting for transfers between devices, swap(): lax.ppermute(value, axis, [(k, k ^ by) for k in range(lax.axis_size(axis))])  77.5 us
    pallas_call x2, Pallas kernels, backward_layer(): pl.pallas_call(functools.partial(backward_kernel, carry is not None, phas...  52.7 us
    ppermute x49, starting transfers between devices, swap(): lax.ppermute(value, axis, [(k, k ^ by) for k in range(lax.axis_size(axis))])  46.4 us
    pallas_call x2, Pallas kernels, forward_layer(): pl.pallas_call(functools.partial(forward_kernel, carry is not None, phase...  44.4 us
    dot_general x8, matrix products, product(): lax.dot_general(a, b, (((0,), (0,)), ((), ())), preferred_element_type=F32)  29.9 us
    ppermute x12, waiting for transfers between devices, block_sends(): lax.ppermute(block_of((rank + k) % count), axis, [(i, (i + k) % count) fo...  25.7 us
    ppermute x3, starting transfers between devices, dp_total(): lax.ppermute(values, 'dp', [(i, (i + k) % count) for i in range(count)])  20 us
    pallas_call x2, Pallas kernels, join(): pl.pallas_call(join_kernel, name='join', out_shape=jax.ShapeDtypeStruct((...  19.4 us
  transfers between devices with their start and end apart: 64, of which 20 were waited for; matrix products, arithmetic and copies ran while one was open for 14% of the time, Pallas kernels for 25%

profile of v1, /device:TPU:0, one launch (start us, length us, event | category | flops | bytes accessed | tf_op | source)
XLA Modules:
  0.0 395.2 jit_solution(16735576212166951901)
XLA Ops:
  1.9 3.1 collective-permute-start.2
  20.6 4.0 %collective-permute-done.3.refs_6_ = bf16[1024,128]{1,0:T(8,128)(2,1)} collective-permute-done((bf16[1024,128]{1,0:T(8,128)(2,1)S(1)}, bf16[1024,128]{1,0:T(8,128)(2,1)}, u32[]{:S(2)}, u32[]{:S(2)}) %collective-permute-start.3) | collective-permute-done | bytes 262176 | tf_op jit(solution)/shard_map/ppermute | solution.py:453
  34.1 22.5 %layer_forward.2 = (bf16[2,1024,128]{2,1,0:T(8,128)(2,1)}, bf16[2,1024,128]{2,1,0:T(8,128)(2,1)}, f32[1024,256]{1,0:T(8,128)}, f32[1024,128]{1,0:T(8,128)}, f32[...) custom-call(s32[2]{0:T(128)} %get-tuple-element.333.refs_0_.meta, ...), custom_call_target="tpu_custom_call" | custom-call | flops 20480000000 | bytes 25165824 | tf_op jit(solution)/shard_map/layer_forward/pallas_call | solution.py:382
  58.1 9.4 %collective-permute-done.11 = bf16[2,1024,128]{2,1,0:T(8,128)(2,1)S(1)} collective-permute-done((bf16[2,1024,128]{2,1,0:T(8,128)(2,1)}, bf16[2,1024,128]{2,1,0:T(8,128)(2,1)S(1)}, u32[]{:S(2)}, u32[]{:S(2)}) %collective-permute-start.11) | collective-permute-done | bytes 524320 | tf_op jit(solution)/shard_map/ppermute | solution.py:453
  71.8 4.0 %collective-permute-done.12 = bf16[1024,128]{1,0:T(8,128)(2,1)S(1)} collective-permute-done((bf16[1024,128]{1,0:T(8,128)(2,1)S(1)}, bf16[1024,128]{1,0:T(8,128)(2,1)S(1)}, u32[]{:S(2)}, u32[]{:S(2)}) %collective-permute-start.12) | collective-permute-done | bytes 262176 | tf_op jit(solution)/shard_map/ppermute | solution.py:453
  80.8 9.2 %collective-permute-done.16.refs_4_ = bf16[1024,256]{1,0:T(8,128)(2,1)S(1)} collective-permute-done((bf16[1024,256]{1,0:T(8,128)(2,1)S(1)}, bf16[1024,256]{1,0:T(8,128)(2,1)S(1)}, u32[]{:S(2)}, u32[]{:S(2)}) %collective-permute-start.16) | collective-permute-done | bytes 524320 | tf_op jit(solution)/shard_map/ppermute | solution.py:453
  95.9 3.6 collective-permute-done.18.refs_6_
  103.1 22.0 %layer_forward.3 = (f32[1024,256]{1,0:T(8,128)}, bf16[1024,256]{1,0:T(8,128)(2,1)}, bf16[1024,256]{1,0:T(8,128)(2,1)}, bf16[1024,256]{1,0:T(8,128)(2,1)}, bf16[1...) custom-call(s32[2]{0:T(128)} %pad_add_fusion.refs_0_.meta, ...), custom_call_target="tpu_custom_call" | custom-call | flops 20480000000 | bytes 25165824 | tf_op jit(solution)/shard_map/layer_forward/pallas_call | solution.py:382
  126.5 3.6 join.2.refs_1_
  130.1 4.8 %convolution_convert_fusion.2 = bf16[640,1024]{1,0:T(8,128)(2,1)} fusion(bf16[1024,1024]{1,0:T(8,128)(2,1)} %join.2.refs_1_, bf16[1024,1280]{1,0:T(8,128)(2,1)} %get-tuple-element.142, s32[]{:T(128)S(6)} %select_n.302), kind=kOutput, calls=%fused_computation.15 | convolution fusion | flops 1342832640 | bytes 4718596 | tf_op jit(solution)/shard_map/dot_general | solution.py:539
  142.7 3.5 collective-permute-start.24
  146.2 3.8 collective-permute-done.25
  151.6 26.6 %layer_backward.2 = (bf16[2,1024,128]{2,1,0:T(8,128)(2,1)}, bf16[2,1024,128]{2,1,0:T(8,128)(2,1)}, f32[1024,256]{1,0:T(8,128)}, f32[1024,128]{1,0:T(8,128)}, f32...) custom-call(s32[2]{0:T(128)} %pad_add_fusion.refs_0_.meta, ...), custom_call_target="tpu_custom_call" | custom-call | flops 25600000000 | bytes 25165824 | tf_op jit(solution)/shard_map/layer_backward/pallas_call | solution.py:422
  181.0 10.9 %collective-permute-done.28 = bf16[2,1024,128]{2,1,0:T(8,128)(2,1)S(1)} collective-permute-done((bf16[2,1024,128]{2,1,0:T(8,128)(2,1)}, bf16[2,1024,128]{2,1,0:T(8,128)(2,1)S(1)}, u32[]{:S(2)}, u32[]{:S(2)}) %collective-permute-start.28) | collective-permute-done | bytes 524320 | tf_op jit(solution)/shard_map/ppermute | solution.py:453
  195.7 5.8 %fusion.11 = bf16[1024,896]{1,0:T(8,128)(2,1)} fusion(bf16[1024,1024]{1,0:T(8,128)(2,1)} %get-tuple-element.144.refs_2_, bf16[1024,1792]{1,0:T(8,128)(2,1)} %get-tuple-element.177, s32[]{:T(128)S(6)} %select_n.311), kind=kOutput, calls=%fused_computation.10 | convolution fusion | flops 1879965696 | bytes 5767172 | tf_op jit(solution)/shard_map/dot_general | solution.py:539
  206.5 4.5 %fusion.8 = bf16[1024,896]{1,0:T(8,128)(2,1)S(1)} fusion(bf16[1024,1024]{1,0:T(8,128)(2,1)} %get-tuple-element.144.refs_2_, bf16[1024,1792]{1,0:T(8,128)(2,1)} %get-tuple-element.177, s32[]{:T(128)S(6)} %select_n.310), kind=kOutput, calls=%fused_computation.9 | convolution fusion | flops 1879965696 | bytes 5767172 | tf_op jit(solution)/shard_map/dot_general | solution.py:539
  215.1 3.8 collective-permute-done.31
  219.6 7.8 %collective-permute-done.36 = bf16[256,896]{1,0:T(8,128)(2,1)S(1)} collective-permute-done((bf16[256,896]{1,0:T(8,128)(2,1)S(1)}, bf16[256,896]{1,0:T(8,128)(2,1)S(1)}, u32[]{:S(2)}, u32[]{:S(2)}) %collective-permute-start.36) | collective-permute-done | bytes 458784 | tf_op jit(solution)/shard_map/ppermute | solution.py:526
  230.1 9.9 %collective-permute-done.38.p2 = bf16[1024,256]{1,0:T(8,128)(2,1)S(1)} collective-permute-done((bf16[1024,256]{1,0:T(8,128)(2,1)S(1)}, bf16[1024,256]{1,0:T(8,128)(2,1)S(1)}, u32[]{:S(2)}, u32[]{:S(2)}) %collective-permute-start.38) | collective-permute-done | bytes 524320 | tf_op jit(solution)/shard_map/ppermute | solution.py:453
  242.5 7.7 %collective-permute-done.41 = bf16[256,896]{1,0:T(8,128)(2,1)S(1)} collective-permute-done((bf16[256,896]{1,0:T(8,128)(2,1)S(1)}, bf16[256,896]{1,0:T(8,128)(2,1)S(1)}, u32[]{:S(2)}, u32[]{:S(2)}) %collective-permute-start.41) | collective-permute-done | bytes 458784 | tf_op jit(solution)/shard_map/ppermute | solution.py:526
  250.3 15.8 %join.3.refs_1_ = bf16[1024,1024]{1,0:T(8,128)(2,1)} custom-call(s32[2]{0:T(128)} %get-tuple-element.333.refs_0_.meta, bf16[1024,256]{1,0:T(8,128)(2,1)} %copy-done.2, bf16[1024,256]{1,0:T(8,128)(2,1)} %copy-done.15, bf16[1024,256]{1,0:T(8,128)(2,1)} %copy-done.14, bf16[1024,128]{1,0:T(8,128)(2,1)} %collective-permute-done.39.p3a, ...), custom_call_target="tpu_custom_call" | custom-call | bytes 4194304 | tf_op jit(solution)/shard_map/join/pallas_call | solution.py:438
  266.0 3.7 convolution_convert_fusion
  272.6 10.2 %collective-permute-done.43 = bf16[256,896]{1,0:T(8,128)(2,1)S(1)} collective-permute-done((bf16[256,896]{1,0:T(8,128)(2,1)S(1)}, bf16[256,896]{1,0:T(8,128)(2,1)S(1)}, u32[]{:S(2)}, u32[]{:S(2)}) %collective-permute-start.43) | collective-permute-done | bytes 458784 | tf_op jit(solution)/shard_map/ppermute | solution.py:526
  287.0 26.1 %layer_backward.3 = (f32[1024,256]{1,0:T(8,128)}, bf16[1024,256]{1,0:T(8,128)(2,1)}, bf16[1024,256]{1,0:T(8,128)(2,1)}, bf16[1024,256]{1,0:T(8,128)(2,1)}, f32[8...) custom-call(s32[2]{0:T(128)} %get-tuple-element.333.refs_0_.meta, ...), custom_call_target="tpu_custom_call" | custom-call | flops 25600000000 | bytes 25165824 | tf_op jit(solution)/shard_map/layer_backward/pallas_call | solution.py:422
  313.3 4.2 %fusion.17 = bf16[1024,896]{1,0:T(8,128)(2,1)S(1)} fusion(bf16[1024,1024]{1,0:T(8,128)(2,1)S(1)} %copy-done.58, bf16[1024,1792]{1,0:T(8,128)(2,1)} %get-tuple-element.212, s32[]{:T(128)S(6)} %select_n.311), kind=kOutput, calls=%fused_computation.12 | convolution fusion | flops 1879965696 | bytes 5767172 | tf_op jit(solution)/shard_map/dot_general | solution.py:539
  337.4 3.3 collective-permute-start.60
  340.7 9.2 %collective-permute-done.48 = bf16[1024,256]{1,0:T(8,128)(2,1)} collective-permute-done((bf16[1024,256]{1,0:T(8,128)(2,1)}, bf16[1024,256]{1,0:T(8,128)(2,1)}, u32[]{:S(2)}, u32[]{:S(2)}) %collective-permute-start.48) | collective-permute-done | bytes 524320 | tf_op jit(solution)/shard_map/ppermute | solution.py:453
  353.9 3.1 select_bitcast_fusion
  357.3 3.2 collective-permute-start.59
  360.6 14.8 %collective-permute-start.58 = (f32[17152]{0:T(1024)S(1)}, f32[17152]{0:T(1024)S(1)}, u32[]{:S(2)}, u32[]{:S(2)}) collective-permute-start(f32[17152]{0:T(1024)S(1)} %select_add_fusion), channel_id=1, source_target_pairs={{0,8},{4,12},{8,0},{12,4},{1,9},{5,13},{9,1},{13,5},{2,10},{6,14},... | collective-permute-start | bytes 205832 | tf_op jit(solution)/shard_map/ppermute | solution.py:516
  377.5 4.2 %collective-permute-done.58 = f32[17152]{0:T(1024)S(1)} collective-permute-done((f32[17152]{0:T(1024)S(1)}, f32[17152]{0:T(1024)S(1)}, u32[]{:S(2)}, u32[]{:S(2)}) %collective-permute-start.58) | collective-permute-done | bytes 68640 | tf_op jit(solution)/shard_map/ppermute | solution.py:516
  391.8 3.2 maximum_select_fusion
  (319 shorter events, 121.7 us)
Async XLA Ops:
  1.9 15.0 %collective-permute-start.2 = (bf16[1024,256]{1,0:T(8,128)(2,1)S(1)}, bf16[1024,256]{1,0:T(8,128)(2,1)S(1)}, u32[]{:S(2)}, u32[]{:S(2)}) collective-permute-start(bf16[1024,256]{1,0:T(8,128)(2,1)S(1)} %dynamic-slice_bitcast_fusion.refs_2_), channel_id=1, source_target_pairs={{0,2},{1,3},{2,0},{3,1},{4,6},{5,7},{6,4},{7,5},{8,10},{9,11},{10,... | collective-permute-start | bytes 1572872 | tf_op jit(solution)/shard_map/ppermute | solution.py:453
  4.9 14.4 %collective-permute-start = (bf16[1024,256]{1,0:T(8,128)(2,1)S(1)}, bf16[1024,256]{1,0:T(8,128)(2,1)}, u32[]{:S(2)}, u32[]{:S(2)}) collective-permute-start(bf16[1024,256]{1,0:T(8,128)(2,1)S(1)} %dynamic-slice_bitcast_fusion.refs_2_), channel_id=1, source_target_pairs={{0,1},{1,0},{2,3},{3,2},{4,5},{5,4},{6,7},{7,6},{8,9},{9,8},{10,11... | collective-permute-start | bytes 1572872 | tf_op jit(solution)/shard_map/ppermute | solution.py:453
  8.9 25.2 %collective-permute-start.6 = (bf16[1,1024,1024]{2,1,0:T(8,128)(2,1)}, bf16[1,1024,1024]{2,1,0:T(8,128)(2,1)}, u32[]{:S(2)}, u32[]{:S(2)}) collective-permute-start(bf16[1,1024,1024]{2,1,0:T(8,128)(2,1)} %refs_19_.3), channel_id=1, source_target_pairs={{0,16},{16,0},{1,17},{17,1},{2,18},{18,2},{3,19},{19,3},{4,20},{20... | collective-permute-start | bytes 6291464 | tf_op jit(solution)/shard_map/ppermute | solution.py:453
  9.4 24.7 %collective-permute-start.8 = (bf16[1,1024,1024]{2,1,0:T(8,128)(2,1)}, bf16[1,1024,1024]{2,1,0:T(8,128)(2,1)}, u32[]{:S(2)}, u32[]{:S(2)}) collective-permute-start(bf16[1,1024,1024]{2,1,0:T(8,128)(2,1)} %refs_21_.3), channel_id=1, source_target_pairs={{0,16},{16,0},{1,17},{17,1},{2,18},{18,2},{3,19},{19,3},{4,20},{20... | collective-permute-start | bytes 6291464 | tf_op jit(solution)/shard_map/ppermute | solution.py:453
  15.0 19.1 %collective-permute-start.5 = (bf16[1,3,1024,256]{3,2,1,0:T(8,128)(2,1)}, bf16[1,3,1024,256]{3,2,1,0:T(8,128)(2,1)}, u32[]{:S(2)}, u32[]{:S(2)}) collective-permute-start(bf16[1,3,1024,256]{3,2,1,0:T(8,128)(2,1)} %refs_18_.3), channel_id=1, source_target_pairs={{0,16},{16,0},{1,17},{17,1},{2,18},{18,2},{3,19},{19,3},{4,20},{20... | collective-permute-start | bytes 4718600 | tf_op jit(solution)/shard_map/ppermute | solution.py:453
  19.3 13.2 %collective-permute-start.7 = (bf16[1,256,1024]{2,1,0:T(8,128)(2,1)}, bf16[1,256,1024]{2,1,0:T(8,128)(2,1)}, u32[]{:S(2)}, u32[]{:S(2)}) collective-permute-start(bf16[1,256,1024]{2,1,0:T(8,128)(2,1)} %refs_20_.3), channel_id=1, source_target_pairs={{0,16},{16,0},{1,17},{17,1},{2,18},{18,2},{3,19},{19,3},{4,20},{20... | collective-permute-start | bytes 1572872 | tf_op jit(solution)/shard_map/ppermute | solution.py:453
  31.4 25.2 %collective-permute-start.10 = (bf16[1024,256]{1,0:T(8,128)(2,1)S(1)}, bf16[1024,256]{1,0:T(8,128)(2,1)S(1)}, u32[]{:S(2)}, u32[]{:S(2)}) collective-permute-start(bf16[1024,256]{1,0:T(8,128)(2,1)S(1)} %dynamic-slice_bitcast_fusion.1.p0), channel_id=1, source_target_pairs={{0,2},{1,3},{2,0},{3,1},{4,6},{5,7},{6,4},{7,5},{8,10},{9,11},{10,... | collective-permute-start | bytes 1572872 | tf_op jit(solution)/shard_map/ppermute | solution.py:453
  32.6 24.0 %collective-permute-start.9 = (bf16[1024,256]{1,0:T(8,128)(2,1)S(1)}, bf16[1024,256]{1,0:T(8,128)(2,1)S(1)}, u32[]{:S(2)}, u32[]{:S(2)}) collective-permute-start(bf16[1024,256]{1,0:T(8,128)(2,1)S(1)} %dynamic-slice_bitcast_fusion.1.p0), channel_id=1, source_target_pairs={{0,1},{1,0},{2,3},{3,2},{4,5},{5,4},{6,7},{7,6},{8,9},{9,8},{10,11... | collective-permute-start | bytes 1572872 | tf_op jit(solution)/shard_map/ppermute | solution.py:453
  101.1 24.0 %collective-permute-start.20 = (bf16[1024,128]{1,0:T(8,128)(2,1)S(1)}, bf16[1024,128]{1,0:T(8,128)(2,1)S(1)}, u32[]{:S(2)}, u32[]{:S(2)}) collective-permute-start(bf16[1024,128]{1,0:T(8,128)(2,1)S(1)} %slice.192), channel_id=1, source_target_pairs={{0,1},{1,0},{2,3},{3,2},{4,5},{5,4},{6,7},{7,6},{8,9},{9,8},{10,11... | collective-permute-start | bytes 786440 | tf_op jit(solution)/shard_map/ppermute | solution.py:453
  101.5 23.6 %collective-permute-start.19 = (bf16[1024,128]{1,0:T(8,128)(2,1)S(1)}, bf16[1024,128]{1,0:T(8,128)(2,1)S(1)}, u32[]{:S(2)}, u32[]{:S(2)}) collective-permute-start(bf16[1024,128]{1,0:T(8,128)(2,1)S(1)} %slice.191), channel_id=1, source_target_pairs={{0,2},{1,3},{2,0},{3,1},{4,6},{5,7},{6,4},{7,5},{8,10},{9,11},{10,... | collective-permute-start | bytes 786440 | tf_op jit(solution)/shard_map/ppermute | solution.py:453
  134.9 15.1 %collective-permute-start.25 = (bf16[1024,256]{1,0:T(8,128)(2,1)}, bf16[1024,256]{1,0:T(8,128)(2,1)}, u32[]{:S(2)}, u32[]{:S(2)}) collective-permute-start(bf16[1024,256]{1,0:T(8,128)(2,1)} %get-tuple-element.164), channel_id=1, source_target_pairs={{0,1},{1,0},{2,3},{3,2},{4,5},{5,4},{6,7},{7,6},{8,9},{9,8},{10,11... | collective-permute-start | bytes 1572872 | tf_op jit(solution)/shard_map/ppermute | solution.py:453
  135.2 43.0 %collective-permute-start.26 = (bf16[1024,256]{1,0:T(8,128)(2,1)}, bf16[1024,256]{1,0:T(8,128)(2,1)}, u32[]{:S(2)}, u32[]{:S(2)}) collective-permute-start(bf16[1024,256]{1,0:T(8,128)(2,1)} %get-tuple-element.165), channel_id=1, source_target_pairs={{0,2},{1,3},{2,0},{3,1},{4,6},{5,7},{6,4},{7,5},{8,10},{9,11},{10,... | collective-permute-start | bytes 1572872 | tf_op jit(solution)/shard_map/ppermute | solution.py:453
  137.0 41.2 %collective-permute-start.27 = (bf16[1024,256]{1,0:T(8,128)(2,1)}, bf16[1024,256]{1,0:T(8,128)(2,1)}, u32[]{:S(2)}, u32[]{:S(2)}) collective-permute-start(bf16[1024,256]{1,0:T(8,128)(2,1)} %get-tuple-element.166), channel_id=1, source_target_pairs={{0,3},{1,2},{2,1},{3,0},{4,7},{5,6},{6,5},{7,4},{8,11},{9,10},{10,... | collective-permute-start | bytes 1572872 | tf_op jit(solution)/shard_map/ppermute | solution.py:453
  142.7 35.5 %collective-permute-start.24 = (bf16[640,256]{1,0:T(8,128)(2,1)S(1)}, bf16[640,256]{1,0:T(8,128)(2,1)S(1)}, u32[]{:S(2)}, u32[]{:S(2)}) collective-permute-start(bf16[640,256]{1,0:T(8,128)(2,1)S(1)} %get-tuple-element.289), channel_id=1, source_target_pairs={{0,12},{4,0},{8,4},{12,8},{1,13},{5,1},{9,5},{13,9},{2,14},{6,2},{... | collective-permute-start | bytes 983048 | tf_op jit(solution)/shard_map/ppermute | solution.py:526
  146.2 32.0 %collective-permute-start.23 = (bf16[640,256]{1,0:T(8,128)(2,1)S(1)}, bf16[640,256]{1,0:T(8,128)(2,1)S(1)}, u32[]{:S(2)}, u32[]{:S(2)}) collective-permute-start(bf16[640,256]{1,0:T(8,128)(2,1)S(1)} %get-tuple-element.290), channel_id=1, source_target_pairs={{0,8},{4,12},{8,0},{12,4},{1,9},{5,13},{9,1},{13,5},{2,10},{6,14},... | collective-permute-start | bytes 983048 | tf_op jit(solution)/shard_map/ppermute | solution.py:526
  150.0 28.3 %collective-permute-start.22 = (bf16[640,256]{1,0:T(8,128)(2,1)S(1)}, bf16[640,256]{1,0:T(8,128)(2,1)S(1)}, u32[]{:S(2)}, u32[]{:S(2)}) collective-permute-start(bf16[640,256]{1,0:T(8,128)(2,1)S(1)} %get-tuple-element.291), channel_id=1, source_target_pairs={{0,4},{4,8},{8,12},{12,0},{1,5},{5,9},{9,13},{13,1},{2,6},{6,10},{... | collective-permute-start | bytes 983048 | tf_op jit(solution)/shard_map/ppermute | solution.py:526
  179.3 14.4 %collective-permute-start.30 = (bf16[2,1024,128]{2,1,0:T(8,128)(2,1)}, bf16[2,1024,128]{2,1,0:T(8,128)(2,1)S(1)}, u32[]{:S(2)}, u32[]{:S(2)}) collective-permute-start(bf16[2,1024,128]{2,1,0:T(8,128)(2,1)} %get-tuple-element.170), channel_id=1, source_target_pairs={{0,2},{1,3},{2,0},{3,1},{4,6},{5,7},{6,4},{7,5},{8,10},{9,11},{10,... | collective-permute-start | bytes 1572872 | tf_op jit(solution)/shard_map/ppermute | solution.py:453
  213.4 13.9 %collective-permute-start.36 = (bf16[256,896]{1,0:T(8,128)(2,1)S(1)}, bf16[256,896]{1,0:T(8,128)(2,1)S(1)}, u32[]{:S(2)}, u32[]{:S(2)}) collective-permute-start(bf16[256,896]{1,0:T(8,128)(2,1)S(1)} %get-tuple-element.283), channel_id=1, source_target_pairs={{0,4},{4,8},{8,12},{12,0},{1,5},{5,9},{9,13},{13,1},{2,6},{6,10},{... | collective-permute-start | bytes 1376264 | tf_op jit(solution)/shard_map/ppermute | solution.py:526
  229.4 20.8 %collective-permute-start.41 = (bf16[256,896]{1,0:T(8,128)(2,1)S(1)}, bf16[256,896]{1,0:T(8,128)(2,1)S(1)}, u32[]{:S(2)}, u32[]{:S(2)}) collective-permute-start(bf16[256,896]{1,0:T(8,128)(2,1)S(1)} %get-tuple-element.282), channel_id=1, source_target_pairs={{0,8},{4,12},{8,0},{12,4},{1,9},{5,13},{9,1},{13,5},{2,10},{6,14},... | collective-permute-start | bytes 1376264 | tf_op jit(solution)/shard_map/ppermute | solution.py:526
  269.7 13.0 %collective-permute-start.42 = (bf16[640,1024]{1,0:T(8,128)(2,1)S(1)}, bf16[640,1024]{1,0:T(8,128)(2,1)S(1)}, u32[]{:S(2)}, u32[]{:S(2)}) collective-permute-start(bf16[640,1024]{1,0:T(8,128)(2,1)S(1)} %convolution_convert_fusion), channel_id=1, source_target_pairs={{0,16},{16,0},{1,17},{17,1},{2,18},{18,2},{3,19},{19,3},{4,20},{20... | collective-permute-start | bytes 3932168 | tf_op jit(solution)/shard_map/ppermute | solution.py:453
  283.5 29.7 %collective-permute-start.46 = (bf16[640,256]{1,0:T(8,128)(2,1)S(1)}, bf16[640,256]{1,0:T(8,128)(2,1)S(1)}, u32[]{:S(2)}, u32[]{:S(2)}) collective-permute-start(bf16[640,256]{1,0:T(8,128)(2,1)S(1)} %get-tuple-element.285), channel_id=1, source_target_pairs={{0,12},{4,0},{8,4},{12,8},{1,13},{5,1},{9,5},{13,9},{2,14},{6,2},{... | collective-permute-start | bytes 983048 | tf_op jit(solution)/shard_map/ppermute | solution.py:526
  286.4 26.8 %collective-permute-start.45 = (bf16[640,256]{1,0:T(8,128)(2,1)S(1)}, bf16[640,256]{1,0:T(8,128)(2,1)S(1)}, u32[]{:S(2)}, u32[]{:S(2)}) collective-permute-start(bf16[640,256]{1,0:T(8,128)(2,1)S(1)} %get-tuple-element.286), channel_id=1, source_target_pairs={{0,8},{4,12},{8,0},{12,4},{1,9},{5,13},{9,1},{13,5},{2,10},{6,14},... | collective-permute-start | bytes 983048 | tf_op jit(solution)/shard_map/ppermute | solution.py:526
  286.4 26.9 %collective-permute-start.44 = (bf16[640,256]{1,0:T(8,128)(2,1)S(1)}, bf16[640,256]{1,0:T(8,128)(2,1)S(1)}, u32[]{:S(2)}, u32[]{:S(2)}) collective-permute-start(bf16[640,256]{1,0:T(8,128)(2,1)S(1)} %get-tuple-element.287), channel_id=1, source_target_pairs={{0,4},{4,8},{8,12},{12,0},{1,5},{5,9},{9,13},{13,1},{2,6},{6,10},{... | collective-permute-start | bytes 983048 | tf_op jit(solution)/shard_map/ppermute | solution.py:526
  320.6 13.4 %collective-permute-start.52 = (f32[8,1024]{1,0:T(8,128)S(1)}, f32[8,1024]{1,0:T(8,128)S(1)}, u32[]{:S(2)}, u32[]{:S(2)}) collective-permute-start(f32[8,1024]{1,0:T(8,128)S(1)} %copy-done.51), channel_id=1, source_target_pairs={{0,1},{1,0},{2,3},{3,2},{4,5},{5,4},{6,7},{7,6},{8,9},{9,8},{10,11... | collective-permute-start | bytes 98312 | tf_op jit(solution)/shard_map/ppermute | solution.py:453
  322.3 15.1 %collective-permute-start.47 = (bf16[1024,256]{1,0:T(8,128)(2,1)}, bf16[1024,256]{1,0:T(8,128)(2,1)}, u32[]{:S(2)}, u32[]{:S(2)}) collective-permute-start(bf16[1024,256]{1,0:T(8,128)(2,1)} %get-tuple-element.208), channel_id=1, source_target_pairs={{0,1},{1,0},{2,3},{3,2},{4,5},{5,4},{6,7},{7,6},{8,9},{9,8},{10,11... | collective-permute-start | bytes 1572872 | tf_op jit(solution)/shard_map/ppermute | solution.py:453
  325.1 24.8 %collective-permute-start.48 = (bf16[1024,256]{1,0:T(8,128)(2,1)}, bf16[1024,256]{1,0:T(8,128)(2,1)}, u32[]{:S(2)}, u32[]{:S(2)}) collective-permute-start(bf16[1024,256]{1,0:T(8,128)(2,1)} %get-tuple-element.209), channel_id=1, source_target_pairs={{0,2},{1,3},{2,0},{3,1},{4,6},{5,7},{6,4},{7,5},{8,10},{9,11},{10,... | collective-permute-start | bytes 1572872 | tf_op jit(solution)/shard_map/ppermute | solution.py:453
  328.1 21.8 %collective-permute-start.49 = (bf16[1024,256]{1,0:T(8,128)(2,1)}, bf16[1024,256]{1,0:T(8,128)(2,1)}, u32[]{:S(2)}, u32[]{:S(2)}) collective-permute-start(bf16[1024,256]{1,0:T(8,128)(2,1)} %get-tuple-element.210), channel_id=1, source_target_pairs={{0,3},{1,2},{2,1},{3,0},{4,7},{5,6},{6,5},{7,4},{8,11},{9,10},{10,... | collective-permute-start | bytes 1572872 | tf_op jit(solution)/shard_map/ppermute | solution.py:453
  329.7 20.2 %collective-permute-start.51 = (bf16[256,896]{1,0:T(8,128)(2,1)}, bf16[256,896]{1,0:T(8,128)(2,1)}, u32[]{:S(2)}, u32[]{:S(2)}) collective-permute-start(bf16[256,896]{1,0:T(8,128)(2,1)} %get-tuple-element.279), channel_id=1, source_target_pairs={{0,4},{4,8},{8,12},{12,0},{1,5},{5,9},{9,13},{13,1},{2,6},{6,10},{... | collective-permute-start | bytes 1376264 | tf_op jit(solution)/shard_map/ppermute | solution.py:526
  334.0 51.5 %collective-permute-start.61 = (bf16[256,896]{1,0:T(8,128)(2,1)}, bf16[256,896]{1,0:T(8,128)(2,1)}, u32[]{:S(2)}, u32[]{:S(2)}) collective-permute-start(bf16[256,896]{1,0:T(8,128)(2,1)} %get-tuple-element.277), channel_id=1, source_target_pairs={{0,12},{4,0},{8,4},{12,8},{1,13},{5,1},{9,5},{13,9},{2,14},{6,2},{... | collective-permute-start | bytes 1376264 | tf_op jit(solution)/shard_map/ppermute | solution.py:526
  337.4 48.1 %collective-permute-start.60 = (bf16[256,896]{1,0:T(8,128)(2,1)}, bf16[256,896]{1,0:T(8,128)(2,1)}, u32[]{:S(2)}, u32[]{:S(2)}) collective-permute-start(bf16[256,896]{1,0:T(8,128)(2,1)} %get-tuple-element.278), channel_id=1, source_target_pairs={{0,8},{4,12},{8,0},{12,4},{1,9},{5,13},{9,1},{13,5},{2,10},{6,14},... | collective-permute-start | bytes 1376264 | tf_op jit(solution)/shard_map/ppermute | solution.py:526
  357.3 20.1 %collective-permute-start.59 = (f32[17152]{0:T(1024)S(1)}, f32[17152]{0:T(1024)S(1)}, u32[]{:S(2)}, u32[]{:S(2)}) collective-permute-start(f32[17152]{0:T(1024)S(1)} %select_add_fusion), channel_id=1, source_target_pairs={{0,12},{4,0},{8,4},{12,8},{1,13},{5,1},{9,5},{13,9},{2,14},{6,2},{... | collective-permute-start | bytes 205832 | tf_op jit(solution)/shard_map/ppermute | solution.py:516
  360.6 21.1 %collective-permute-start.58 = (f32[17152]{0:T(1024)S(1)}, f32[17152]{0:T(1024)S(1)}, u32[]{:S(2)}, u32[]{:S(2)}) collective-permute-start(f32[17152]{0:T(1024)S(1)} %select_add_fusion), channel_id=1, source_target_pairs={{0,8},{4,12},{8,0},{12,4},{1,9},{5,13},{9,1},{13,5},{2,10},{6,14},... | collective-permute-start | bytes 205832 | tf_op jit(solution)/shard_map/ppermute | solution.py:516
  (91 other events, 916.4 us)

commit v2 on v1

--- a/solution.py
+++ b/solution.py
@@ -313,6 +313,10 @@
     stats[...] = totals[0] + totals[1] + totals[2] + totals[3]
 
 
+def product_kernel(which, left, right, out):
+    out[...] = dot_tn(left[...], right[...]).astype(BF16)
+
+
 def join_kernel(meta, p0, p1, p2, p3a, p3b, whole):
     half = LANES // 2
     for r, piece in enumerate((p0, p1, p2)):
@@ -343,8 +347,8 @@
     return [pl.BlockSpec(memory_space=pl.ANY)] * count
 
 
-def params(axes=1):
-    return pltpu.CompilerParams(dimension_semantics=("arbitrary",) * axes, vmem_limit_bytes=56 << 20)
+def params(size):
+    return pltpu.CompilerParams(dimension_semantics=("arbitrary",), vmem_limit_bytes=size << 20)
 
 
 def weight_scratch(width):
@@ -386,7 +390,7 @@
         grid_spec=pltpu.PrefetchScalarGridSpec(
             num_scalar_prefetch=2, grid=(tiles,), in_specs=in_specs, out_specs=specs, scratch_shapes=weight_scratch(width)),
         input_output_aliases=aliases,
-        compiler_params=params(),
+        compiler_params=params(32),
         cost_estimate=pl.CostEstimate(flops=rows * 20_000_000, transcendentals=rows * 5000, bytes_accessed=24 << 20),
     )(*operands)
     count = 5 if phased else 4
@@ -426,7 +430,7 @@
         grid_spec=pltpu.PrefetchScalarGridSpec(
             num_scalar_prefetch=1, grid=(tiles,), in_specs=in_specs, out_specs=specs, scratch_shapes=weight_scratch(width)),
         input_output_aliases=aliases,
-        compiler_params=params(),
+        compiler_params=params(32),
         cost_estimate=pl.CostEstimate(flops=rows * 25_000_000, transcendentals=0, bytes_accessed=24 << 20),
     )(*operands)
     count = 5 if phased else 4
@@ -445,6 +449,7 @@
             in_specs=[pl.BlockSpec((block, p.shape[1]), lambda i, *_: (i, 0)) for p in pieces],
             out_specs=pl.BlockSpec((block, 4 * LANES), lambda i, *_: (i, 0)),
         ),
+        compiler_params=params(8),
         cost_estimate=pl.CostEstimate(flops=0, transcendentals=0, bytes_accessed=rows * 16 * LANES),
     )(meta, *pieces)
 
@@ -506,7 +511,7 @@
     for step in range(2, count + 1):
         arrived = lax.ppermute(total, axis, pairs)
         total = (arrived.astype(F32) + block_of((rank + count - step) % count).astype(F32)).astype(BF16)
-    return total
+        yield arrived, total
 
 
 def dp_total(values):
@@ -521,7 +526,7 @@
     count = lax.axis_size(axis)
     rank = lax.axis_index(axis)
     if count > 8:
-        return [ring_scatter(block_of, axis)]
+        return [list(ring_scatter(block_of, axis))[-1][1]]
     return [block_of(rank)] + [
         lax.ppermute(block_of((rank + k) % count), axis, [(i, (i + k) % count) for i in range(count)]) for k in range(1, count)]
 
@@ -533,13 +538,29 @@
     return total.astype(BF16)
 
 
-def weight_gradient(left, right, half_of, section, *before_own):
-    def product(which, *before):
-        a, b = half_of(left, after(right, *before), which)
-        return lax.dot_general(a, b, (((0,), (0,)), ((), ())), preferred_element_type=F32).astype(BF16)
+def weight_gradient(left, right, cut_left, section):
+    rows = left.shape[0]
+    m, n = left.shape[1] // (2 if cut_left else 1), right.shape[1] // (1 if cut_left else 2)
+    block = 128 if cut_left else 256
+    steps = m // block
+    left_at = (lambda i, which: (0, which[0] * steps + i)) if cut_left else (lambda i, which: (0, i))
+    right_at = (lambda i, which: (0, 0)) if cut_left else (lambda i, which: (0, which[0]))
+
+    def product(which):
+        return pl.pallas_call(
+            product_kernel,
+            name="weight_gradient",
+            out_shape=jax.ShapeDtypeStruct((m, n), BF16),
+            grid_spec=pltpu.PrefetchScalarGridSpec(
+                num_scalar_prefetch=1, grid=(steps,),
+                in_specs=[pl.BlockSpec((rows, block), left_at), pl.BlockSpec((rows, n), right_at)],
+                out_specs=pl.BlockSpec((block, n), lambda i, which: (i, 0))),
+            compiler_params=params(20),
+            cost_estimate=pl.CostEstimate(flops=2 * rows * m * n, transcendentals=0, bytes_accessed=2 * (rows * (m + n) + m * n)),
+        )(which.reshape(1).astype(jnp.int32), left, right)
 
     arrived = swap(product(1 - section), "section", 1)
-    return lax.optimization_barrier(product(section, *before_own)), arrived
+    return product(section), arrived
 
 
 def dct_table(order):
@@ -617,14 +638,6 @@
     def saved_of(arrays):
         return (arrays[0],) + tuple(arrays[3:])
 
-    def in_half(left, right, which):
-        n = right.shape[1] // 2
-        return left, lax.dynamic_slice_in_dim(right, which * n, n, 1)
-
-    def out_half(left, right, which):
-        n = left.shape[1] // 2
-        return lax.dynamic_slice_in_dim(left, which * n, n, 1), right
-
     def in_block(mine, arrived):
         n = mine.shape[0] // groups
         cut = lambda v, i: lax.dynamic_slice_in_dim(v, i * n, n, 0)
@@ -654,33 +667,34 @@
 
     saved1, saved0 = saved_of(all1), saved_of(all0)
     grad1 = join(metas[1], pieces_g)
-    out_blocks1 = block_sends(out_block(*weight_gradient(saved1[6], grad1, out_half, section)), "dp")
+    out_blocks1 = block_sends(out_block(*weight_gradient(saved1[6], grad1, True, section)), "dp")
     grad1_b = after(grad1, out_blocks1[0])
     parts, stats, dcat1, dmix1, fsum1 = run_backward(metas[1], grad1_b, saved1, weights1, True)
     parts, stats, dcat1, dmix1, fsum1 = after((parts, stats, dcat1, dmix1, fsum1), *out_blocks1, *out_sent)
     arrived = scatter_start(parts)
     turn = scatter_turn(parts, arrived)
     sums = mp_total(after(stats, *turn))
-    dcat1 = after(dcat1, *turn)
-    in_blocks1 = block_sends(in_block(*weight_gradient(saved1[0], dcat1, in_half, section)), "dp")
+    steps1 = list(ring_scatter(in_block(*weight_gradient(saved1[0], dcat1, False, section)), "dp"))
+    arrivals1, red_in1 = [arrival for arrival, _ in steps1], steps1[-1][1]
     d_normed = scatter_end(parts, arrived, *turn)
     g0 = norm_backward(cot, d_normed, sums, all1[1:3], weights1[0][0]).astype(BF16)
     small1 = small_gradients(d_normed, all1[1:3], dmix1, fsum1)
-    pieces_g0 = after(gather_pieces(after(g0, *in_blocks1[:2])), *in_blocks1[:3])
+    pieces_g0 = gather_pieces(after(g0, arrivals1[0]), arrivals1[1:2])
+    pieces_g0 = after(pieces_g0, *arrivals1[2:3])
     out = hidden.astype(F32) + out_kept + out_sent[0].astype(F32) + out_sent[1].astype(F32) + out_sent[2].astype(F32)
 
     grad0 = join(metas[0], pieces_g0)
-    mine0, arrived0 = after(weight_gradient(saved0[6], grad0, out_half, section), *in_blocks1)
-    out_blocks0 = block_sends(out_block(mine0, arrived0), "dp")
+    out_blocks0 = block_sends(out_block(*weight_gradient(saved0[6], grad0, True, section)), "dp")
     grad0_b = after(grad0, out_blocks0[0])
     parts, stats, dcat0, dmix0, fsum0 = run_backward(metas[0], grad0_b, saved0, weights0, False)
     parts, stats, dcat0, dmix0, fsum0 = after((parts, stats, dcat0, dmix0, fsum0), *out_blocks0)
-    out_blocks1, in_blocks1 = after((out_blocks1, in_blocks1), dcat0)
+    out_blocks1 = after(out_blocks1, dcat0)
     kept, sent = direct_sends(parts)
     sums = mp_total(stats)
-    mine0, arrived0 = weight_gradient(saved0[0], dcat0, in_half, section)
-    in_blocks0 = block_sends(in_block(mine0, arrived0), "dp")
-    sent, dmix0, out_blocks0, out_blocks1, in_blocks1 = after((sent, dmix0, out_blocks0, out_blocks1, in_blocks1), *in_blocks0[:2])
+    mine0, arrived0 = weight_gradient(saved0[0], dcat0, False, section)
+    block0 = in_block(mine0, arrived0)
+    steps0 = list(ring_scatter(block0, "dp"))
+    sent, dmix0, out_blocks0, out_blocks1 = after((sent, dmix0, out_blocks0, out_blocks1), steps0[0][0])
     d_normed = kept + sent[0].astype(F32) + sent[1].astype(F32) + sent[2].astype(F32)
     d_input = norm_backward(g0, d_normed, sums, all0[1:3], weights0[0][0])
     small0 = small_gradients(d_normed, all0[1:3], dmix0, fsum0)
@@ -691,7 +705,6 @@
         return jnp.where(is_first, jnp.concatenate([mine, arrived], axis), jnp.concatenate([arrived, mine], axis)).astype(F32)
 
     grads_out = to_owner(sum_blocks(out_blocks0), sum_blocks(out_blocks1), 0)
-    red_in1 = sum_blocks(in_blocks1)
     small_mine, small_send = both(small0, small1)
     small_sum = dp_total(small_mine + swap(small_send, "section", 1))
     feat_grad = small_sum[2 * shard_width:2 * shard_width + LANES].reshape(heads, HEAD) / feat_weight[0]
@@ -700,8 +713,7 @@
     keep, send = both(d_input, out)
     arrived = swap(send, "section", 1)
     boundary = jnp.where(is_first, jnp.stack([keep, arrived]), jnp.stack([arrived, keep]))
-    in_blocks0 = after(in_blocks0, grads_out, small_sum, boundary, red_in1)
-    grads_in = to_owner(sum_blocks(in_blocks0), red_in1, 1)
+    grads_in = to_owner(steps0[-1][1], red_in1, 1)
     qkv_grad = jnp.stack([grads_in[:, t * shard_width:(t + 1) * shard_width] for t in range(3)])
     return (
         boundary[None],

time: 399 us -> 407 us (1.020)
  local copies, waits for them, and re-layouts: 20.3 us -> 64.9 us
  matrix products: 31.2 us -> 2.68 us
  starting transfers between devices: 85.7 us -> 61.2 us
  waiting for transfers between devices: 107 us -> 115 us
  other arithmetic: 32 us -> 36.2 us
    unnamed x119 -> x277, local copies, waits for them, and re-layouts: 4.02 us -> 39.9 us
    ppermute x0 -> x6, waiting for transfers between devices: none -> 31.4 us  [ring_scatter(): arrived = lax.ppermute(total, axis, pairs)]
    dot_general x8 -> x0, matrix products: 29.9 us -> none  [product(): lax.dot_general(a, b, (((0,), (0,)), ((), ())), preferred_element_type=F32)]
    pallas_call x0 -> x8, Pallas kernels: none -> 27.3 us  [product(): pl.pallas_call(product_kernel, name='weight_gradient', out_shape=jax.Shap...]
    ppermute x12 -> x6, waiting for transfers between devices: 25.7 us -> 3.58 us  [block_sends(): lax.ppermute(block_of((rank + k) % count), axis, [(i, (i + k) % count) fo...]
    pallas_call x2, Pallas kernels: 19.4 us -> 1.86 us  [join(): pl.pallas_call(join_kernel, name='join', out_shape=jax.ShapeDtypeStruct((...]
    ppermute x3, starting transfers between devices: 20 us -> 4.04 us  [dp_total(): lax.ppermute(values, 'dp', [(i, (i + k) % count) for i in range(count)])]
    ppermute x12 -> x6, starting transfers between devices: 19.2 us -> 7.98 us  [block_sends(): lax.ppermute(block_of((rank + k) % count), axis, [(i, (i + k) % count) fo...]
  transfers between devices with their start and end apart: 64 -> 64, of which waited for: 20 -> 25; matrix products, arithmetic and copies ran while one was open for 14% -> 14% of each run, Pallas kernels for 25% -> 25%
where the time goes in v2:
time: 407 us; the launch traced here: 401 us
  Pallas kernels  118 us (29%)
  waiting for transfers between devices  115 us (28%)
  local copies, waits for them, and re-layouts  64.9 us (16%)
  starting transfers between devices  61.2 us (15%)
  other arithmetic  36.2 us (9%)
    ppermute x49, waiting for transfers between devices, swap(): lax.ppermute(value, axis, [(k, k ^ by) for k in range(lax.axis_size(axis))])  67.6 us
    pallas_call x2, Pallas kernels, backward_layer(): pl.pallas_call(functools.partial(backward_kernel, carry is not None, phas...  47.9 us
    ppermute x49, starting transfers between devices, swap(): lax.ppermute(value, axis, [(k, k ^ by) for k in range(lax.axis_size(axis))])  44.9 us
    pallas_call x2, Pallas kernels, forward_layer(): pl.pallas_call(functools.partial(forward_kernel, carry is not None, phase...  40.9 us
    unnamed x277, local copies, waits for them, and re-layouts  39.9 us
    ppermute x6, waiting for transfers between devices, ring_scatter(): arrived = lax.ppermute(total, axis, pairs)  31.4 us
    pallas_call x8, Pallas kernels, product(): pl.pallas_call(product_kernel, name='weight_gradient', out_shape=jax.Shap...  27.3 us
    ppermute x3, waiting for transfers between devices, dp_total(): lax.ppermute(values, 'dp', [(i, (i + k) % count) for i in range(count)])  12.5 us
  transfers between devices with their start and end apart: 64, of which 25 were waited for; matrix products, arithmetic and copies ran while one was open for 14% of the time, Pallas kernels for 25%

profile of v2, /device:TPU:0, one launch (start us, length us, event | category | flops | bytes accessed | tf_op | source)
XLA Modules:
  0.0 401.0 jit_solution(10097490943617558176)
XLA Ops:
  1.9 3.1 collective-permute-start.2
  33.7 4.6 %collective-permute-done.1.refs_5_ = bf16[1024,128]{1,0:T(8,128)(2,1)S(1)} collective-permute-done((bf16[1024,128]{1,0:T(8,128)(2,1)}, bf16[1024,128]{1,0:T(8,128)(2,1)S(1)}, u32[]{:S(2)}, u32[]{:S(2)}) %collective-permute-start.1) | collective-permute-done | bytes 262176 | tf_op jit(solution)/shard_map/ppermute | solution.py:458
  44.1 20.6 %layer_forward.2 = (bf16[2,1024,128]{2,1,0:T(8,128)(2,1)S(1)}, bf16[2,1024,128]{2,1,0:T(8,128)(2,1)S(1)}, f32[1024,256]{1,0:T(8,128)S(1)}, f32[1024,128]{1,0:T(8...) custom-call(s32[2]{0:T(128)S(1)} %get-tuple-element.300.refs_0_.meta, ...), custom_call_target="tpu_custom_call" | custom-call | flops 20480000000 | bytes 25165824 | tf_op jit(solution)/shard_map/layer_forward/pallas_call | solution.py:386
  73.3 11.0 %collective-permute-done.11 = bf16[2,1024,128]{2,1,0:T(8,128)(2,1)S(1)} collective-permute-done((bf16[2,1024,128]{2,1,0:T(8,128)(2,1)S(1)}, bf16[2,1024,128]{2,1,0:T(8,128)(2,1)S(1)}, u32[]{:S(2)}, u32[]{:S(2)}) %collective-permute-start.11) | collective-permute-done | bytes 524320 | tf_op jit(solution)/shard_map/ppermute | solution.py:458
  86.5 4.6 %collective-permute-done.12 = bf16[1024,128]{1,0:T(8,128)(2,1)S(1)} collective-permute-done((bf16[1024,128]{1,0:T(8,128)(2,1)S(1)}, bf16[1024,128]{1,0:T(8,128)(2,1)S(1)}, u32[]{:S(2)}, u32[]{:S(2)}) %collective-permute-start.12) | collective-permute-done | bytes 262176 | tf_op jit(solution)/shard_map/ppermute | solution.py:458
  94.8 8.6 %collective-permute-done.16.refs_4_ = bf16[1024,256]{1,0:T(8,128)(2,1)} collective-permute-done((bf16[1024,256]{1,0:T(8,128)(2,1)S(1)}, bf16[1024,256]{1,0:T(8,128)(2,1)}, u32[]{:S(2)}, u32[]{:S(2)}) %collective-permute-start.16) | collective-permute-done | bytes 524320 | tf_op jit(solution)/shard_map/ppermute | solution.py:458
  113.0 2.8 collective-permute-done.17.refs_5_
  118.9 20.3 %layer_forward.3 = (f32[1024,256]{1,0:T(8,128)S(1)}, bf16[1024,256]{1,0:T(8,128)(2,1)}, bf16[1024,256]{1,0:T(8,128)(2,1)}, bf16[1024,256]{1,0:T(8,128)(2,1)S(1)}...) custom-call(s32[2]{0:T(128)S(1)} %pad_add_fusion.refs_0_.meta, ...), custom_call_target="tpu_custom_call" | custom-call | flops 20480000000 | bytes 25165824 | tf_op jit(solution)/shard_map/layer_forward/pallas_call | solution.py:386
  151.7 3.7 weight_gradient.9
  160.7 2.7 weight_gradient.8
  163.5 2.7 add_convert_fusion.21
  166.2 3.8 collective-permute-start.24
  175.3 24.1 %layer_backward.2 = (bf16[2,1024,128]{2,1,0:T(8,128)(2,1)}, bf16[2,1024,128]{2,1,0:T(8,128)(2,1)}, f32[1024,256]{1,0:T(8,128)S(1)}, f32[1024,128]{1,0:T(8,128)S(...) custom-call(s32[2]{0:T(128)S(1)} %pad_add_fusion.refs_0_.meta, ...), custom_call_target="tpu_custom_call" | custom-call | flops 25600000000 | bytes 25165824 | tf_op jit(solution)/shard_map/layer_backward/pallas_call | solution.py:426
  199.5 3.3 copy-done.4
  202.8 4.3 %weight_gradient.11 = bf16[1024,896]{1,0:T(8,128)(2,1)} custom-call(s32[1]{0:T(128)} %bitcast.21.which, bf16[1024,1024]{1,0:T(8,128)(2,1)S(1)} %copy-done.12, bf16[1024,1792]{1,0:T(8,128)(2,1)S(1)} %copy-done.4), custom_call_target="tpu_custom_call" | custom-call | flops 1879048192 | bytes 5767168 | tf_op jit(solution)/shard_map/weight_gradient/pallas_call | solution.py:550
  211.4 3.4 weight_gradient.10
  214.8 7.2 %collective-permute-done.28 = bf16[2,1024,128]{2,1,0:T(8,128)(2,1)} collective-permute-done((bf16[2,1024,128]{2,1,0:T(8,128)(2,1)}, bf16[2,1024,128]{2,1,0:T(8,128)(2,1)}, u32[]{:S(2)}, u32[]{:S(2)}) %collective-permute-start.28) | collective-permute-done | bytes 524320 | tf_op jit(solution)/shard_map/ppermute | solution.py:458
  232.7 9.2 %collective-permute-done.36 = bf16[256,896]{1,0:T(8,128)(2,1)S(1)} collective-permute-done((bf16[256,896]{1,0:T(8,128)(2,1)S(1)}, bf16[256,896]{1,0:T(8,128)(2,1)S(1)}, u32[]{:S(2)}, u32[]{:S(2)}) %collective-permute-start.36) | collective-permute-done | bytes 458784 | tf_op jit(solution)/shard_map/ppermute | solution.py:512
  247.0 8.0 %collective-permute-done.39 = bf16[256,896]{1,0:T(8,128)(2,1)S(1)} collective-permute-done((bf16[256,896]{1,0:T(8,128)(2,1)S(1)}, bf16[256,896]{1,0:T(8,128)(2,1)S(1)}, u32[]{:S(2)}, u32[]{:S(2)}) %collective-permute-start.39) | collective-permute-done | bytes 458784 | tf_op jit(solution)/shard_map/ppermute | solution.py:512
  260.8 3.6 collective-permute-done.41.p3b
  268.2 2.7 weight_gradient.13
  271.1 2.7 weight_gradient.12
  278.2 23.8 %layer_backward.3 = (f32[1024,256]{1,0:T(8,128)S(1)}, bf16[1024,256]{1,0:T(8,128)(2,1)S(1)}, bf16[1024,256]{1,0:T(8,128)(2,1)}, bf16[1024,256]{1,0:T(8,128)(2,1)...) custom-call(s32[2]{0:T(128)S(1)} %get-tuple-element.300.refs_0_.meta, ...), custom_call_target="tpu_custom_call" | custom-call | flops 25600000000 | bytes 25165824 | tf_op jit(solution)/shard_map/layer_backward/pallas_call | solution.py:426
  302.1 3.6 collective-permute-done.45
  308.0 4.2 %weight_gradient.15 = bf16[1024,896]{1,0:T(8,128)(2,1)} custom-call(s32[1]{0:T(128)} %bitcast.21.which, bf16[1024,1024]{1,0:T(8,128)(2,1)S(1)} %copy-done.10, bf16[1024,1792]{1,0:T(8,128)(2,1)S(1)} %copy-done.2), custom_call_target="tpu_custom_call" | custom-call | flops 1879048192 | bytes 5767168 | tf_op jit(solution)/shard_map/weight_gradient/pallas_call | solution.py:550
  319.7 3.5 weight_gradient.14
  331.9 16.2 %collective-permute-done.48 = bf16[1024,256]{1,0:T(8,128)(2,1)} collective-permute-done((bf16[1024,256]{1,0:T(8,128)(2,1)}, bf16[1024,256]{1,0:T(8,128)(2,1)}, u32[]{:S(2)}, u32[]{:S(2)}) %collective-permute-start.48) | collective-permute-done | bytes 524320 | tf_op jit(solution)/shard_map/ppermute | solution.py:458
  355.2 2.3 collective-permute-start.59
  361.4 8.1 %collective-permute-done.59 = f32[17152]{0:T(1024)S(1)} collective-permute-done((f32[17152]{0:T(1024)S(1)}, f32[17152]{0:T(1024)S(1)}, u32[]{:S(2)}, u32[]{:S(2)}) %collective-permute-start.59) | collective-permute-done | bytes 68640 | tf_op jit(solution)/shard_map/ppermute | solution.py:521
  369.5 4.4 %collective-permute-done.58 = f32[17152]{0:T(1024)S(1)} collective-permute-done((f32[17152]{0:T(1024)S(1)}, f32[17152]{0:T(1024)S(1)}, u32[]{:S(2)}, u32[]{:S(2)}) %collective-permute-start.58) | collective-permute-done | bytes 68640 | tf_op jit(solution)/shard_map/ppermute | solution.py:521
  379.2 12.4 %collective-permute-done.61 = bf16[256,896]{1,0:T(8,128)(2,1)S(1)} collective-permute-done((bf16[256,896]{1,0:T(8,128)(2,1)S(1)}, bf16[256,896]{1,0:T(8,128)(2,1)S(1)}, u32[]{:S(2)}, u32[]{:S(2)}) %collective-permute-start.61) | collective-permute-done | bytes 458784 | tf_op jit(solution)/shard_map/ppermute | solution.py:512
  395.2 3.1 maximum_select_fusion
  (480 shorter events, 159.4 us)
Async XLA Ops:
  1.9 15.1 %collective-permute-start.2 = (bf16[1024,256]{1,0:T(8,128)(2,1)S(1)}, bf16[1024,256]{1,0:T(8,128)(2,1)}, u32[]{:S(2)}, u32[]{:S(2)}) collective-permute-start(bf16[1024,256]{1,0:T(8,128)(2,1)S(1)} %dynamic-slice_bitcast_fusion.refs_2_), channel_id=1, source_target_pairs={{0,2},{1,3},{2,0},{3,1},{4,6},{5,7},{6,4},{7,5},{8,10},{9,11},{10,... | collective-permute-start | bytes 1572872 | tf_op jit(solution)/shard_map/ppermute | solution.py:458
  4.9 19.9 %collective-permute-start = (bf16[1024,256]{1,0:T(8,128)(2,1)S(1)}, bf16[1024,256]{1,0:T(8,128)(2,1)}, u32[]{:S(2)}, u32[]{:S(2)}) collective-permute-start(bf16[1024,256]{1,0:T(8,128)(2,1)S(1)} %dynamic-slice_bitcast_fusion.refs_2_), channel_id=1, source_target_pairs={{0,1},{1,0},{2,3},{3,2},{4,5},{5,4},{6,7},{7,6},{8,9},{9,8},{10,11... | collective-permute-start | bytes 1572872 | tf_op jit(solution)/shard_map/ppermute | solution.py:458
  8.9 32.2 %collective-permute-start.6 = (bf16[1,1024,1024]{2,1,0:T(8,128)(2,1)}, bf16[1,1024,1024]{2,1,0:T(8,128)(2,1)}, u32[]{:S(2)}, u32[]{:S(2)}) collective-permute-start(bf16[1,1024,1024]{2,1,0:T(8,128)(2,1)} %refs_19_.3), channel_id=1, source_target_pairs={{0,16},{16,0},{1,17},{17,1},{2,18},{18,2},{3,19},{19,3},{4,20},{20... | collective-permute-start | bytes 6291464 | tf_op jit(solution)/shard_map/ppermute | solution.py:458
  9.4 31.7 %collective-permute-start.8 = (bf16[1,1024,1024]{2,1,0:T(8,128)(2,1)}, bf16[1,1024,1024]{2,1,0:T(8,128)(2,1)}, u32[]{:S(2)}, u32[]{:S(2)}) collective-permute-start(bf16[1,1024,1024]{2,1,0:T(8,128)(2,1)} %refs_21_.3), channel_id=1, source_target_pairs={{0,16},{16,0},{1,17},{17,1},{2,18},{18,2},{3,19},{19,3},{4,20},{20... | collective-permute-start | bytes 6291464 | tf_op jit(solution)/shard_map/ppermute | solution.py:458
  13.7 27.4 %collective-permute-start.5 = (bf16[1,3,1024,256]{3,2,1,0:T(8,128)(2,1)}, bf16[1,3,1024,256]{3,2,1,0:T(8,128)(2,1)}, u32[]{:S(2)}, u32[]{:S(2)}) collective-permute-start(bf16[1,3,1024,256]{3,2,1,0:T(8,128)(2,1)} %refs_18_.3), channel_id=1, source_target_pairs={{0,16},{16,0},{1,17},{17,1},{2,18},{18,2},{3,19},{19,3},{4,20},{20... | collective-permute-start | bytes 4718600 | tf_op jit(solution)/shard_map/ppermute | solution.py:458
  24.8 15.7 %collective-permute-start.7 = (bf16[1,256,1024]{2,1,0:T(8,128)(2,1)S(1)}, bf16[1,256,1024]{2,1,0:T(8,128)(2,1)}, u32[]{:S(2)}, u32[]{:S(2)}) collective-permute-start(bf16[1,256,1024]{2,1,0:T(8,128)(2,1)S(1)} %copy-done.51), channel_id=1, source_target_pairs={{0,16},{16,0},{1,17},{17,1},{2,18},{18,2},{3,19},{19,3},{4,20},{20... | collective-permute-start | bytes 1572872 | tf_op jit(solution)/shard_map/ppermute | solution.py:458
  39.0 32.2 %collective-permute-start.10 = (bf16[1024,256]{1,0:T(8,128)(2,1)S(1)}, bf16[1024,256]{1,0:T(8,128)(2,1)S(1)}, u32[]{:S(2)}, u32[]{:S(2)}) collective-permute-start(bf16[1024,256]{1,0:T(8,128)(2,1)S(1)} %dynamic-slice_bitcast_fusion.1.p0), channel_id=1, source_target_pairs={{0,2},{1,3},{2,0},{3,1},{4,6},{5,7},{6,4},{7,5},{8,10},{9,11},{10,... | collective-permute-start | bytes 1572872 | tf_op jit(solution)/shard_map/ppermute | solution.py:458
  40.6 30.7 %collective-permute-start.9 = (bf16[1024,256]{1,0:T(8,128)(2,1)S(1)}, bf16[1024,256]{1,0:T(8,128)(2,1)S(1)}, u32[]{:S(2)}, u32[]{:S(2)}) collective-permute-start(bf16[1024,256]{1,0:T(8,128)(2,1)S(1)} %dynamic-slice_bitcast_fusion.1.p0), channel_id=1, source_target_pairs={{0,1},{1,0},{2,3},{3,2},{4,5},{5,4},{6,7},{7,6},{8,9},{9,8},{10,11... | collective-permute-start | bytes 1572872 | tf_op jit(solution)/shard_map/ppermute | solution.py:458
  115.8 32.5 %collective-permute-start.20 = (bf16[1024,128]{1,0:T(8,128)(2,1)S(1)}, bf16[1024,128]{1,0:T(8,128)(2,1)S(1)}, u32[]{:S(2)}, u32[]{:S(2)}) collective-permute-start(bf16[1024,128]{1,0:T(8,128)(2,1)S(1)} %slice.192), channel_id=1, source_target_pairs={{0,1},{1,0},{2,3},{3,2},{4,5},{5,4},{6,7},{7,6},{8,9},{9,8},{10,11... | collective-permute-start | bytes 786440 | tf_op jit(solution)/shard_map/ppermute | solution.py:458
  117.0 31.3 %collective-permute-start.19 = (bf16[1024,128]{1,0:T(8,128)(2,1)S(1)}, bf16[1024,128]{1,0:T(8,128)(2,1)S(1)}, u32[]{:S(2)}, u32[]{:S(2)}) collective-permute-start(bf16[1024,128]{1,0:T(8,128)(2,1)S(1)} %slice.191), channel_id=1, source_target_pairs={{0,2},{1,3},{2,0},{3,1},{4,6},{5,7},{6,4},{7,5},{8,10},{9,11},{10,... | collective-permute-start | bytes 786440 | tf_op jit(solution)/shard_map/ppermute | solution.py:458
  155.4 15.0 %collective-permute-start.25 = (bf16[1024,256]{1,0:T(8,128)(2,1)}, bf16[1024,256]{1,0:T(8,128)(2,1)S(1)}, u32[]{:S(2)}, u32[]{:S(2)}) collective-permute-start(bf16[1024,256]{1,0:T(8,128)(2,1)} %get-tuple-element.151), channel_id=1, source_target_pairs={{0,1},{1,0},{2,3},{3,2},{4,5},{5,4},{6,7},{7,6},{8,9},{9,8},{10,11... | collective-permute-start | bytes 1572872 | tf_op jit(solution)/shard_map/ppermute | solution.py:458
  157.4 42.0 %collective-permute-start.26 = (bf16[1024,256]{1,0:T(8,128)(2,1)}, bf16[1024,256]{1,0:T(8,128)(2,1)S(1)}, u32[]{:S(2)}, u32[]{:S(2)}) collective-permute-start(bf16[1024,256]{1,0:T(8,128)(2,1)} %get-tuple-element.152), channel_id=1, source_target_pairs={{0,2},{1,3},{2,0},{3,1},{4,6},{5,7},{6,4},{7,5},{8,10},{9,11},{10,... | collective-permute-start | bytes 1572872 | tf_op jit(solution)/shard_map/ppermute | solution.py:458
  157.5 41.9 %collective-permute-start.27 = (bf16[1024,256]{1,0:T(8,128)(2,1)}, bf16[1024,256]{1,0:T(8,128)(2,1)S(1)}, u32[]{:S(2)}, u32[]{:S(2)}) collective-permute-start(bf16[1024,256]{1,0:T(8,128)(2,1)} %copy-done.56), channel_id=1, source_target_pairs={{0,3},{1,2},{2,1},{3,0},{4,7},{5,6},{6,5},{7,4},{8,11},{9,10},{10,... | collective-permute-start | bytes 1572872 | tf_op jit(solution)/shard_map/ppermute | solution.py:458
  166.2 33.3 %collective-permute-start.24 = (bf16[640,256]{1,0:T(8,128)(2,1)S(1)}, bf16[640,256]{1,0:T(8,128)(2,1)S(1)}, u32[]{:S(2)}, u32[]{:S(2)}) collective-permute-start(bf16[640,256]{1,0:T(8,128)(2,1)S(1)} %get-tuple-element.256), channel_id=1, source_target_pairs={{0,12},{4,0},{8,4},{12,8},{1,13},{5,1},{9,5},{13,9},{2,14},{6,2},{... | collective-permute-start | bytes 983048 | tf_op jit(solution)/shard_map/ppermute | solution.py:531
  170.0 29.5 %collective-permute-start.23 = (bf16[640,256]{1,0:T(8,128)(2,1)S(1)}, bf16[640,256]{1,0:T(8,128)(2,1)S(1)}, u32[]{:S(2)}, u32[]{:S(2)}) collective-permute-start(bf16[640,256]{1,0:T(8,128)(2,1)S(1)} %get-tuple-element.257), channel_id=1, source_target_pairs={{0,8},{4,12},{8,0},{12,4},{1,9},{5,13},{9,1},{13,5},{2,10},{6,14},... | collective-permute-start | bytes 983048 | tf_op jit(solution)/shard_map/ppermute | solution.py:531
  170.4 29.0 %collective-permute-start.22 = (bf16[640,256]{1,0:T(8,128)(2,1)S(1)}, bf16[640,256]{1,0:T(8,128)(2,1)S(1)}, u32[]{:S(2)}, u32[]{:S(2)}) collective-permute-start(bf16[640,256]{1,0:T(8,128)(2,1)S(1)} %get-tuple-element.258), channel_id=1, source_target_pairs={{0,4},{4,8},{8,12},{12,0},{1,5},{5,9},{9,13},{13,1},{2,6},{6,10},{... | collective-permute-start | bytes 983048 | tf_op jit(solution)/shard_map/ppermute | solution.py:531
  207.1 20.9 %collective-permute-start.35 = (bf16[1024,896]{1,0:T(8,128)(2,1)}, bf16[1024,896]{1,0:T(8,128)(2,1)}, u32[]{:S(2)}, u32[]{:S(2)}) collective-permute-start(bf16[1024,896]{1,0:T(8,128)(2,1)} %weight_gradient.11), channel_id=1, source_target_pairs={{0,16},{16,0},{1,17},{17,1},{2,18},{18,2},{3,19},{19,3},{4,20},{20... | collective-permute-start | bytes 5505032 | tf_op jit(solution)/shard_map/ppermute | solution.py:458
  207.2 14.8 %collective-permute-start.28 = (bf16[2,1024,128]{2,1,0:T(8,128)(2,1)}, bf16[2,1024,128]{2,1,0:T(8,128)(2,1)}, u32[]{:S(2)}, u32[]{:S(2)}) collective-permute-start(bf16[2,1024,128]{2,1,0:T(8,128)(2,1)} %get-tuple-element.155), channel_id=1, source_target_pairs={{0,1},{1,0},{2,3},{3,2},{4,5},{5,4},{6,7},{7,6},{8,9},{9,8},{10,11... | collective-permute-start | bytes 1572872 | tf_op jit(solution)/shard_map/ppermute | solution.py:458
  209.2 14.3 %collective-permute-start.30 = (bf16[2,1024,128]{2,1,0:T(8,128)(2,1)}, bf16[2,1024,128]{2,1,0:T(8,128)(2,1)}, u32[]{:S(2)}, u32[]{:S(2)}) collective-permute-start(bf16[2,1024,128]{2,1,0:T(8,128)(2,1)} %get-tuple-element.157), channel_id=1, source_target_pairs={{0,2},{1,3},{2,0},{3,1},{4,6},{5,7},{6,4},{7,5},{8,10},{9,11},{10,... | collective-permute-start | bytes 1572872 | tf_op jit(solution)/shard_map/ppermute | solution.py:458
  275.5 26.6 %collective-permute-start.46 = (bf16[640,256]{1,0:T(8,128)(2,1)S(1)}, bf16[640,256]{1,0:T(8,128)(2,1)S(1)}, u32[]{:S(2)}, u32[]{:S(2)}) collective-permute-start(bf16[640,256]{1,0:T(8,128)(2,1)S(1)} %get-tuple-element.252), channel_id=1, source_target_pairs={{0,12},{4,0},{8,4},{12,8},{1,13},{5,1},{9,5},{13,9},{2,14},{6,2},{... | collective-permute-start | bytes 983048 | tf_op jit(solution)/shard_map/ppermute | solution.py:531
  277.5 28.1 %collective-permute-start.45 = (bf16[640,256]{1,0:T(8,128)(2,1)S(1)}, bf16[640,256]{1,0:T(8,128)(2,1)S(1)}, u32[]{:S(2)}, u32[]{:S(2)}) collective-permute-start(bf16[640,256]{1,0:T(8,128)(2,1)S(1)} %get-tuple-element.253), channel_id=1, source_target_pairs={{0,8},{4,12},{8,0},{12,4},{1,9},{5,13},{9,1},{13,5},{2,10},{6,14},... | collective-permute-start | bytes 983048 | tf_op jit(solution)/shard_map/ppermute | solution.py:531
  277.5 28.1 %collective-permute-start.44 = (bf16[640,256]{1,0:T(8,128)(2,1)S(1)}, bf16[640,256]{1,0:T(8,128)(2,1)S(1)}, u32[]{:S(2)}, u32[]{:S(2)}) collective-permute-start(bf16[640,256]{1,0:T(8,128)(2,1)S(1)} %get-tuple-element.254), channel_id=1, source_target_pairs={{0,4},{4,8},{8,12},{12,0},{1,5},{5,9},{9,13},{13,1},{2,6},{6,10},{... | collective-permute-start | bytes 983048 | tf_op jit(solution)/shard_map/ppermute | solution.py:531
  316.8 15.1 %collective-permute-start.47 = (bf16[1024,256]{1,0:T(8,128)(2,1)}, bf16[1024,256]{1,0:T(8,128)(2,1)}, u32[]{:S(2)}, u32[]{:S(2)}) collective-permute-start(bf16[1024,256]{1,0:T(8,128)(2,1)} %copy-done.57), channel_id=1, source_target_pairs={{0,1},{1,0},{2,3},{3,2},{4,5},{5,4},{6,7},{7,6},{8,9},{9,8},{10,11... | collective-permute-start | bytes 1572872 | tf_op jit(solution)/shard_map/ppermute | solution.py:458
  323.3 24.8 %collective-permute-start.48 = (bf16[1024,256]{1,0:T(8,128)(2,1)}, bf16[1024,256]{1,0:T(8,128)(2,1)}, u32[]{:S(2)}, u32[]{:S(2)}) collective-permute-start(bf16[1024,256]{1,0:T(8,128)(2,1)} %get-tuple-element.195), channel_id=1, source_target_pairs={{0,2},{1,3},{2,0},{3,1},{4,6},{5,7},{6,4},{7,5},{8,10},{9,11},{10,... | collective-permute-start | bytes 1572872 | tf_op jit(solution)/shard_map/ppermute | solution.py:458
  326.4 21.6 %collective-permute-start.49 = (bf16[1024,256]{1,0:T(8,128)(2,1)}, bf16[1024,256]{1,0:T(8,128)(2,1)}, u32[]{:S(2)}, u32[]{:S(2)}) collective-permute-start(bf16[1024,256]{1,0:T(8,128)(2,1)} %get-tuple-element.196), channel_id=1, source_target_pairs={{0,3},{1,2},{2,1},{3,0},{4,7},{5,6},{6,5},{7,4},{8,11},{9,10},{10,... | collective-permute-start | bytes 1572872 | tf_op jit(solution)/shard_map/ppermute | solution.py:458
  328.7 19.3 %collective-permute-start.51 = (bf16[256,896]{1,0:T(8,128)(2,1)}, bf16[256,896]{1,0:T(8,128)(2,1)}, u32[]{:S(2)}, u32[]{:S(2)}) collective-permute-start(bf16[256,896]{1,0:T(8,128)(2,1)} %add_convert_fusion.9), channel_id=1, source_target_pairs={{0,4},{4,8},{8,12},{12,0},{1,5},{5,9},{9,13},{13,1},{2,6},{6,10},{... | collective-permute-start | bytes 1376264 | tf_op jit(solution)/shard_map/ppermute | solution.py:512
  351.7 26.3 %collective-permute-start.63 = (bf16[640,256]{1,0:T(8,128)(2,1)}, bf16[640,256]{1,0:T(8,128)(2,1)}, u32[]{:S(2)}, u32[]{:S(2)}) collective-permute-start(bf16[640,256]{1,0:T(8,128)(2,1)} %broadcast_select_fusion.3), channel_id=1, source_target_pairs={{0,16},{16,0},{1,17},{17,1},{2,18},{18,2},{3,19},{19,3},{4,20},{20... | collective-permute-start | bytes 983048 | tf_op jit(solution)/shard_map/ppermute | solution.py:458
  353.6 22.4 %collective-permute-start.60 = (bf16[256,896]{1,0:T(8,128)(2,1)S(1)}, bf16[256,896]{1,0:T(8,128)(2,1)}, u32[]{:S(2)}, u32[]{:S(2)}) collective-permute-start(bf16[256,896]{1,0:T(8,128)(2,1)S(1)} %add_convert_fusion.7), channel_id=1, source_target_pairs={{0,4},{4,8},{8,12},{12,0},{1,5},{5,9},{9,13},{13,1},{2,6},{6,10},{... | collective-permute-start | bytes 1376264 | tf_op jit(solution)/shard_map/ppermute | solution.py:512
  357.5 16.4 %collective-permute-start.58 = (f32[17152]{0:T(1024)S(1)}, f32[17152]{0:T(1024)S(1)}, u32[]{:S(2)}, u32[]{:S(2)}) collective-permute-start(f32[17152]{0:T(1024)S(1)} %select_add_fusion), channel_id=1, source_target_pairs={{0,8},{4,12},{8,0},{12,4},{1,9},{5,13},{9,1},{13,5},{2,10},{6,14},... | collective-permute-start | bytes 205832 | tf_op jit(solution)/shard_map/ppermute | solution.py:521
  359.2 14.7 %collective-permute-start.57 = (f32[17152]{0:T(1024)S(1)}, f32[17152]{0:T(1024)S(1)}, u32[]{:S(2)}, u32[]{:S(2)}) collective-permute-start(f32[17152]{0:T(1024)S(1)} %select_add_fusion), channel_id=1, source_target_pairs={{0,4},{4,8},{8,12},{12,0},{1,5},{5,9},{9,13},{13,1},{2,6},{6,10},{... | collective-permute-start | bytes 205832 | tf_op jit(solution)/shard_map/ppermute | solution.py:521
  369.4 25.8 %collective-permute-start.55 = (f32[1024,256]{1,0:T(8,128)}, f32[1024,256]{1,0:T(8,128)}, u32[]{:S(2)}, u32[]{:S(2)}) collective-permute-start(f32[1024,256]{1,0:T(8,128)} %get-tuple-element.251), channel_id=1, source_target_pairs={{0,16},{16,0},{1,17},{17,1},{2,18},{18,2},{3,19},{19,3},{4,20},{20... | collective-permute-start | bytes 3145736 | tf_op jit(solution)/shard_map/ppermute | solution.py:458
  377.3 14.3 %collective-permute-start.61 = (bf16[256,896]{1,0:T(8,128)(2,1)S(1)}, bf16[256,896]{1,0:T(8,128)(2,1)S(1)}, u32[]{:S(2)}, u32[]{:S(2)}) collective-permute-start(bf16[256,896]{1,0:T(8,128)(2,1)S(1)} %add_convert_fusion.5), channel_id=1, source_target_pairs={{0,4},{4,8},{8,12},{12,0},{1,5},{5,9},{9,13},{13,1},{2,6},{6,10},{... | collective-permute-start | bytes 1376264 | tf_op jit(solution)/shard_map/ppermute | solution.py:512
  (170 other events, 1742.6 us)
